TPU v7x, 128 devices: a whole 4x4x4 slice. The times are simulated.
128 devices in a mesh: tm: 32 (over y, x, core), obj: 4 (over z).
Axes of the slice: x: 4, y: 4, z: 4, core: 2. Of those that a mesh axis runs over, the one named last changes fastest.
Arguments:
- objective: float32 [128, 768, 768], P('tm', 'obj'), parts along dimension 1, may hold values from -6 to 6
- jacobians: bfloat16 [128, 768, 768], P('tm'), may hold values from -0.21875 to 0.21875
- precond_blocks: bfloat16 [2, 128, 768, 768], P(None, 'tm'), as said below
Outputs:
- adjoint: float32 [128, 768, 768], P('tm', 'obj'), parts along dimension 1
- residual: float32 [128, 768, 768], P('tm', 'obj'), parts along dimension 1
There are 4 independent parts, one for each index of `obj`. A program takes and returns all parts, laid end to end along the dimension named above; an argument that names none is the same for every part. Nothing has to cross between parts.
Inputs may be any that keep to these rules, and one draw needn't show every extreme that they name: precond_blocks[0, j] equals precond_blocks[0, (128 - j) mod 128] and precond_blocks[1, j] equals - precond_blocks[1, (128 - j) mod 128].
All inputs are finite; a program needn't handle non-finite values.
Results may differ from a plain program's by a relative error of at most 0.0087.
Values may be sent and summed in bfloat16 or wider, within the bound.
No kernel may reach another device: no remote copies, remote signals or barrier semaphores. Data moves between devices by JAX's collectives and lax.ppermute only.
A program may use at most 128 MiB of HBM per device.

v0:
```python
import math

import jax
import jax.numpy as jnp
import numpy as np
from jax import lax
from jax.sharding import PartitionSpec as P

ITERS = 2
log_alpha = math.log(0.05)


def split_table(table):
    high = table.astype(jnp.bfloat16)
    low = (table - high.astype(np.float64)).astype(jnp.bfloat16)
    return high, low


def tables(steps, groups):
    times = np.arange(steps)
    forward = np.zeros((2, groups, 4, 2, steps))
    backward = np.zeros((2, steps, 2, groups, 4))
    grow = np.exp(times * (-log_alpha / steps))
    shrink = np.exp(times * (log_alpha / steps)) / steps
    for group in range(groups):
        low_side = group < groups // 2
        for position in range(2):
            first = (0 if low_side else 1) ^ position
            jobs = [(0, 4 * group + 1, position), (2, 4 * group + 2 * position, first)]
            for slot, frequency, half in jobs:
                angle = 2.0 * math.pi * ((frequency * times) % steps) / steps
                cosine, sine = np.cos(angle), np.sin(angle)
                if frequency % (steps // 2) == 0:
                    for at, part in ((slot, half), (slot + 1, 1 - half)):
                        forward[position, group, at, part] = cosine * grow
                        backward[part, :, position, group, at] = cosine * shrink
                    continue
                forward[position, group, slot, half] = cosine * grow
                forward[position, group, slot + 1, half] = -sine * grow
                backward[half, :, position, group, slot] = 2.0 * cosine * shrink
                backward[half, :, position, group, slot + 1] = -2.0 * sine * shrink
    size = 2 * steps
    return forward.reshape(size, size), backward.reshape(size, size)


def exchange(block):
    return lax.all_to_all(block, "tm", split_axis=0, concat_axis=0, tiled=True)


def transform(pair, rows):
    high, low = pair
    return jnp.dot(high, rows, preferred_element_type=jnp.float32) + jnp.dot(
        low, rows, preferred_element_type=jnp.float32
    )


def mul(left, right):
    return jnp.dot(left, right, preferred_element_type=jnp.float32)


def body(objective, jacobians, precond_blocks):
    local_steps, columns, states = objective.shape
    groups = lax.axis_size("tm")
    steps = local_steps * groups
    per_piece = columns // groups
    third = per_piece // 2
    forward, backward = tables(steps, groups)
    forward, backward = split_table(forward), split_table(backward)
    real, imag = precond_blocks[0], precond_blocks[1]
    route = [(i + 1, i) for i in range(groups - 1)]
    adjoint = None
    residual = objective
    for _ in range(ITERS):
        send = residual.astype(jnp.bfloat16).transpose(1, 0, 2)
        pieces = exchange(send).reshape(groups, 2, third, local_steps, states)
        rows = pieces.transpose(1, 0, 3, 2, 4).reshape(2 * steps, third * states)
        spectrum = transform(forward, rows).astype(jnp.bfloat16)
        spectrum = spectrum.reshape(2, groups, 4, third, states).transpose(1, 0, 3, 2, 4)
        spectrum = exchange(spectrum.reshape(columns, 4, states))
        spectrum = spectrum.reshape(groups, 2, third, 4, states).transpose(3, 1, 0, 2, 4)
        wave = []
        one_re = spectrum[0].reshape(columns, states)
        one_im = spectrum[1].reshape(columns, states)
        w_re = mul(one_re, real[1]) - mul(one_im, imag[1])
        w_im = mul(one_re, imag[1]) + mul(one_im, real[1])
        shape = (1, 2, groups, third, states)
        wave += [w_re.astype(jnp.bfloat16).reshape(shape), w_im.astype(jnp.bfloat16).reshape(shape)]
        other = [[], []]
        for position in range(2):
            x_re = spectrum[2, position].reshape(columns // 2, states)
            x_im = spectrum[3, position].reshape(columns // 2, states)
            b_re, b_im = real[2 * position], imag[2 * position]
            other[0].append((mul(x_re, b_re) - mul(x_im, b_im)).astype(jnp.bfloat16))
            other[1].append((mul(x_re, b_im) + mul(x_im, b_re)).astype(jnp.bfloat16))
        wave += [jnp.stack(part).reshape(shape) for part in other]
        wave = jnp.concatenate(wave, axis=0).transpose(2, 1, 3, 0, 4)
        wave = exchange(wave.reshape(columns, 4, states))
        rows = wave.reshape(groups, 2, third, 4, states).transpose(1, 0, 3, 2, 4)
        values = transform(backward, rows.reshape(2 * steps, third * states))
        values = values.astype(jnp.bfloat16).reshape(2, groups, local_steps, third, states)
        values = values.transpose(1, 0, 3, 2, 4).reshape(columns, local_steps, states)
        correction = exchange(values).transpose(1, 0, 2)
        next_row = lax.ppermute(correction[:1], "tm", route)
        following = jnp.concatenate([correction[1:], next_row], axis=0)
        carried = jnp.einsum(
            "kcn,knm->kcm", following, jacobians, preferred_element_type=jnp.float32
        )
        correction = correction.astype(jnp.float32)
        adjoint = correction if adjoint is None else adjoint + correction
        residual = residual - (correction - carried)
    return (adjoint, residual)


def solution(mesh):
    in_specs = (P("tm", "obj", None), P("tm", None, None), P(None, "tm", None, None))
    out_specs = (P("tm", "obj", None), P("tm", "obj", None))
    return jax.shard_map(body, mesh=mesh, in_specs=in_specs, out_specs=out_specs, check_vma=False)
```

profile of v0, /device:TPU:1, one launch (start us, length us, event | category | flops | bytes accessed | tf_op | source)
XLA Modules:
  0.0 330.0 jit_solution(15558556691302099319)
XLA Ops:
  3.3 27.2 %all_to_all.40 = bf16[192,4,768]{2,1,0:T(4,128)(2,1)S(1)} all-to-all(bf16[192,4,768]{2,1,0:T(4,128)(2,1)S(1)} %bitcast.221), channel_id=1, replica_groups=mesh['tm'=32,'obj'=4] {'tm'}, dimensions={0} | all-to-all | bytes 2359296 | tf_op jit(solution)/shard_map/all_to_all | solution.py:47
  34.5 2.3 reshape.110
  37.4 22.5 %all_to_all.41 = bf16[192,4,768]{2,1,0:T(4,128)(2,1)S(1)} all-to-all(bf16[192,4,768]{2,1,0:T(4,128)(2,1)S(1)} %bitcast.225), channel_id=1, replica_groups=mesh['tm'=32,'obj'=4] {'tm'}, dimensions={0} | all-to-all | bytes 2359296 | tf_op jit(solution)/shard_map/all_to_all | solution.py:47
  85.3 22.5 %all_to_all.42 = bf16[192,4,768]{2,1,0:T(4,128)(2,1)S(1)} all-to-all(bf16[192,4,768]{2,1,0:T(4,128)(2,1)S(1)} %bitcast.227), channel_id=1, replica_groups=mesh['tm'=32,'obj'=4] {'tm'}, dimensions={0} | all-to-all | bytes 2359296 | tf_op jit(solution)/shard_map/all_to_all | solution.py:47
  112.6 22.5 %all_to_all.43 = bf16[192,4,768]{2,1,0:T(4,128)(2,1)S(1)} all-to-all(bf16[192,4,768]{2,1,0:T(4,128)(2,1)S(1)} %bitcast.229), channel_id=1, replica_groups=mesh['tm'=32,'obj'=4] {'tm'}, dimensions={0} | all-to-all | bytes 2359296 | tf_op jit(solution)/shard_map/all_to_all | solution.py:47
  135.2 2.4 collective-permute-start
  137.7 5.7 %collective-permute-done = bf16[1,192,768]{2,1,0:T(8,128)(2,1)S(1)} collective-permute-done((bf16[1,192,768]{2,1,0:T(8,128)(2,1)S(1)}, bf16[1,192,768]{2,1,0:T(8,128)(2,1)S(1)}, u32[]{:S(2)}, u32[]{:S(2)}) %collective-permute-start) | collective-permute-done | bytes 294944 | tf_op jit(solution)/shard_map/ppermute | solution.py:103
  143.4 3.6 %fusion.7 = f32[4,192,768]{2,1,0:T(8,128)S(1)} fusion(f32[4,192,768]{2,1,0:T(8,128)S(1)} %copy-done, bf16[4,768,768]{2,1,0:T(8,128)(2,1)} %param.8, bf16[1,192,768]{2,1,0:T(8,128)(2,1)S(1)} %collective-permute-done, bf16[3,192,768]{2,1,0:T(8,128)(2,1)S(1)} %slice.118, bf16[192,4,768]{2,1,0:T(4,128)(2,1)S(1)} %all_to_all.43), kind=kOutput, calls=%fused_computation.14 | convolution fusion | flops 908328960 | bytes 11796480 | tf_op jit(solution)/shard_map/kcn,knm->kcm/dot_general | solution.py:105
  148.0 23.6 %all_to_all.44 = bf16[192,4,768]{2,1,0:T(4,128)(2,1)S(1)} all-to-all(bf16[192,4,768]{2,1,0:T(4,128)(2,1)S(1)} %copy.39), channel_id=1, replica_groups=mesh['tm'=32,'obj'=4] {'tm'}, dimensions={0} | all-to-all | bytes 2359296 | tf_op jit(solution)/shard_map/all_to_all | solution.py:47
  175.6 2.4 copy.41
  178.0 3.7 %reshape.122 = bf16[2,32,4,3,768]{4,3,2,1,0:T(4,128)(2,1)} reshape(bf16[256,2304]{1,0:T(8,128)(2,1)} %copy.41) | data formatting | bytes 2359296 | tf_op jit(solution)/shard_map/reshape | solution.py:78
  183.6 22.5 %all_to_all.45 = bf16[192,4,768]{2,1,0:T(4,128)(2,1)S(1)} all-to-all(bf16[192,4,768]{2,1,0:T(4,128)(2,1)S(1)} %bitcast.231), channel_id=1, replica_groups=mesh['tm'=32,'obj'=4] {'tm'}, dimensions={0} | all-to-all | bytes 2359296 | tf_op jit(solution)/shard_map/all_to_all | solution.py:47
  210.9 2.6 fusion.51
  213.5 2.5 fusion.58
  216.0 2.0 reshape_squeeze.43
  226.5 2.3 fusion.37
  228.9 2.3 fusion.99
  232.8 2.4 fusion.102
  238.5 2.3 fusion.21
  240.9 2.3 fusion.87
  244.8 2.4 fusion.90
  248.8 2.6 fusion.12
  253.3 2.6 fusion.11
  257.7 2.7 maximum_bitcast_fusion.1
  262.0 22.5 %all_to_all.46 = bf16[192,4,768]{2,1,0:T(4,128)(2,1)S(1)} all-to-all(bf16[192,4,768]{2,1,0:T(4,128)(2,1)S(1)} %bitcast.233), channel_id=1, replica_groups=mesh['tm'=32,'obj'=4] {'tm'}, dimensions={0} | all-to-all | bytes 2359296 | tf_op jit(solution)/shard_map/all_to_all | solution.py:47
  288.4 2.4 copy.46
  290.8 3.7 %reshape.130 = bf16[2,32,4,3,768]{4,3,2,1,0:T(4,128)(2,1)} reshape(bf16[256,2304]{1,0:T(8,128)(2,1)} %copy.46) | data formatting | bytes 2359296 | tf_op jit(solution)/shard_map/reshape | solution.py:100
  294.5 2.1 copy.47
  296.5 22.5 %all_to_all.47 = bf16[192,4,768]{2,1,0:T(4,128)(2,1)S(1)} all-to-all(bf16[192,4,768]{2,1,0:T(4,128)(2,1)S(1)} %bitcast.235), channel_id=1, replica_groups=mesh['tm'=32,'obj'=4] {'tm'}, dimensions={0} | all-to-all | bytes 2359296 | tf_op jit(solution)/shard_map/all_to_all | solution.py:47
  319.2 2.3 collective-permute-start.1
  323.2 4.1 %collective-permute-done.1 = bf16[1,192,768]{2,1,0:T(8,128)(2,1)S(1)} collective-permute-done((bf16[1,192,768]{2,1,0:T(8,128)(2,1)S(1)}, bf16[1,192,768]{2,1,0:T(8,128)(2,1)S(1)}, u32[]{:S(2)}, u32[]{:S(2)}) %collective-permute-start.1) | collective-permute-done | bytes 294944 | tf_op jit(solution)/shard_map/ppermute | solution.py:103
  327.3 2.7 fusion.8
  (107 shorter events, 76.9 us)
Async XLA Ops:
  31.2 0.9 copy-start.8
  32.1 0.9 copy-start.10
  108.4 0.9 copy-start.6
  109.3 0.9 copy-start.4
  135.2 8.2 %copy-start = (f32[4,192,768]{2,1,0:T(8,128)S(1)}, f32[4,192,768]{2,1,0:T(8,128)}, u32[]{:S(2)}) copy-start(f32[4,192,768]{2,1,0:T(8,128)} %param.7) | copy-start | bytes 7077892
  135.2 8.2 %collective-permute-start = (bf16[1,192,768]{2,1,0:T(8,128)(2,1)S(1)}, bf16[1,192,768]{2,1,0:T(8,128)(2,1)S(1)}, u32[]{:S(2)}, u32[]{:S(2)}) collective-permute-start(bf16[1,192,768]{2,1,0:T(8,128)(2,1)S(1)} %slice.119), channel_id=1, source_target_pairs={{4,0},{8,4},{12,8},{16,12},{20,16},{24,20},{28,24},{32,28},{36,32}... | collective-permute-start | bytes 884744 | tf_op jit(solution)/shard_map/ppermute | solution.py:103
  172.3 0.9 copy-start.9
  173.2 0.9 copy-start.11
  210.9 2.6 copy-start.1
  224.8 1.7 copy-start.3
  236.8 1.7 copy-start.2
  285.1 0.9 copy-start.7
  286.0 0.9 copy-start.5
  294.5 32.8 %slice-start = ((s8[4718592]{0:T(1024)(128)(4,1)}), s8[4194304]{0:T(1024)(128)(4,1)S(1)}, s32[]{:S(2)}) async-start(s8[4718592]{0:T(1024)(128)(4,1)} %bitcast.197), calls=%async_computation.8 | async-start | bytes 8388608
  319.0 8.3 %slice-start.1 = ((s8[4718592]{0:T(1024)(128)(4,1)}), s8[524288]{0:T(1024)(128)(4,1)S(1)}, s32[]{:S(2)}) async-start(s8[4718592]{0:T(1024)(128)(4,1)} %bitcast.197), calls=%async_computation.9 | async-start | bytes 1048576
  319.2 8.0 %collective-permute-start.1 = (bf16[1,192,768]{2,1,0:T(8,128)(2,1)S(1)}, bf16[1,192,768]{2,1,0:T(8,128)(2,1)S(1)}, u32[]{:S(2)}, u32[]{:S(2)}) collective-permute-start(bf16[1,192,768]{2,1,0:T(8,128)(2,1)S(1)} %slice.127), channel_id=1, source_target_pairs={{4,0},{8,4},{12,8},{16,12},{20,16},{24,20},{28,24},{32,28},{36,32}... | collective-permute-start | bytes 884744 | tf_op jit(solution)/shard_map/ppermute | solution.py:103
where the time goes:
time: 332 us; the launch traced here: 330 us
  blocking collectives  186 us (56%)
  matrix products  60.6 us (18%)
  local copies, waits for them, and re-layouts  60.2 us (18%)
  waiting for transfers between devices  9.75 us (3%)
  other arithmetic  7.71 us (2%)
  starting transfers between devices  4.76 us (1%)
    all_to_all x8, blocking collectives, exchange(): return lax.all_to_all(block, 'tm', split_axis=0, concat_axis=0, tiled=True)  186 us
    dot_general x24, matrix products, mul(): return jnp.dot(left, right, preferred_element_type=jnp.float32)  47.2 us
    ppermute x2, waiting for transfers between devices, body(): next_row = lax.ppermute(correction[:1], 'tm', route)  9.75 us
    another operation x8, local copies, waits for them, and re-layouts, body(): wave += [jnp.stack(part).reshape(shape) for part in other]  6.95 us
  transfers between devices with their start and end apart: 2, of which 2 were waited for; matrix products, arithmetic and copies ran while one was open for 1% of the time, Pallas kernels for 0%

commit v1 on v0

v1 whole, which is shorter than its diff:
```python
import functools
import math

import jax
import jax.numpy as jnp
import numpy as np
from jax import lax
from jax.experimental import pallas as pl
from jax.experimental.pallas import tpu as pltpu
from jax.sharding import PartitionSpec as P

ITERS = 2
log_alpha = math.log(0.05)
MIB = 1 << 20


def split_table(table):
    high = table.astype(jnp.bfloat16)
    low = (table - high.astype(np.float64)).astype(jnp.bfloat16)
    return np.concatenate([high, low], axis=1)


def tables(steps, groups):
    local = steps // groups
    times = np.arange(steps)
    forward = np.zeros((groups, 2, 4, 2, steps))
    backward = np.zeros((2, steps, groups, 2, 4))
    grow = np.exp(times * (-log_alpha / steps))
    shrink = np.exp(times * (log_alpha / steps)) / steps
    for group in range(groups):
        low_side = group < groups // 2
        for position in range(2):
            first = (0 if low_side else 1) ^ position
            jobs = [(0, 4 * group + 1, position), (2, 4 * group + 2 * position, first)]
            for slot, frequency, half in jobs:
                angle = 2.0 * math.pi * ((frequency * times) % steps) / steps
                cosine, sine = np.cos(angle), np.sin(angle)
                if frequency % (steps // 2) == 0:
                    for at, part in ((slot, half), (slot + 1, 1 - half)):
                        forward[group, position, at, part] = cosine * grow
                        backward[part, :, group, position, at] = cosine * shrink
                    continue
                forward[group, position, slot, half] = cosine * grow
                forward[group, position, slot + 1, half] = -sine * grow
                backward[half, :, group, position, slot] = 2.0 * cosine * shrink
                backward[half, :, group, position, slot + 1] = -2.0 * sine * shrink
    size = 2 * steps
    forward = forward.reshape(size, 2, groups, local).transpose(0, 2, 1, 3)
    backward = backward.reshape(2, groups, local, size).transpose(1, 0, 2, 3)
    return forward.reshape(size, size), backward.reshape(size, size)


def shuffles(groups):
    size = 8 * groups
    pack = np.zeros((groups, 2, 4, 4, 2, groups))
    sort = np.zeros((4, 2, groups, groups, 2, 4))
    for piece in range(groups):
        for half in range(2):
            for step in range(4):
                pack[piece, half, step, step, half, piece] = 1
                sort[step, half, piece, piece, half, step] = 1
    shape = (size, size)
    return pack.reshape(shape).astype(jnp.bfloat16), sort.reshape(shape).astype(jnp.bfloat16)


def mul(left, right):
    return jnp.dot(left, right, preferred_element_type=jnp.float32)


def rows_of(ref, third):
    groups, _, eight, states = ref.shape
    wide = ref[:, third].astype(jnp.float32)
    return wide.reshape(groups * eight, states).astype(jnp.bfloat16)


def put_rows(ref, third, rows):
    groups, _, eight, states = ref.shape
    ref[:, third] = rows.reshape(groups, eight, states).astype(ref.dtype)


def pack_kernel(block_ref, pack_ref, send_ref):
    steps, columns, states = block_ref.shape
    rows = block_ref[...].reshape(steps * columns, states).astype(jnp.bfloat16)
    put_rows(send_ref, 0, mul(pack_ref[...], rows))


def transform_kernel(in_ref, table_ref, out_ref):
    for third in range(in_ref.shape[1]):
        rows = rows_of(in_ref, third)
        put_rows(out_ref, third, mul(table_ref[...], jnp.concatenate([rows, rows], axis=0)))


def multiply_kernel(in_ref, sort_ref, unsort_ref, blocks_ref, out_ref, held, sorted_ref, sem):
    groups, thirds, _, states = in_ref.shape
    copies = []
    for index, frequency in enumerate((1, 0, 2)):
        for part in range(2):
            copies.append(
                pltpu.make_async_copy(
                    blocks_ref.at[part, frequency], held.at[index, part], sem.at[index, part]
                )
            )
            copies[-1].start()
    half = thirds * groups
    for third in range(thirds):
        rows = mul(sort_ref[...], rows_of(in_ref, third)).astype(jnp.bfloat16)
        for block in range(8):
            at = block * half + third * groups
            sorted_ref[at : at + groups] = rows[block * groups : (block + 1) * groups]
    for copy in copies[:2]:
        copy.wait()

    def product(index, rows, length):
        left = sorted_ref[rows : rows + length]
        count = length // 2
        y = mul(left, held[index, 0])
        z = mul(left, held[index, 1])
        sorted_ref[rows : rows + count] = (y[:count] - z[count:]).astype(jnp.bfloat16)
        sorted_ref[rows + count : rows + length] = (z[:count] + y[count:]).astype(jnp.bfloat16)

    def pair_product(index, re_at, im_at):
        left = jnp.concatenate(
            [sorted_ref[re_at : re_at + half], sorted_ref[im_at : im_at + half]], axis=0
        )
        y = mul(left, held[index, 0])
        z = mul(left, held[index, 1])
        sorted_ref[re_at : re_at + half] = (y[:half] - z[half:]).astype(jnp.bfloat16)
        sorted_ref[im_at : im_at + half] = (z[:half] + y[half:]).astype(jnp.bfloat16)

    product(0, 0, 4 * half)
    for index in (1, 2):
        for copy in copies[2 * index : 2 * index + 2]:
            copy.wait()
        pair_product(index, (4 + index - 1) * half, (6 + index - 1) * half)
    for third in range(thirds):
        at = third * groups
        rows = [sorted_ref[block * half + at : block * half + at + groups] for block in range(8)]
        put_rows(out_ref, third, mul(unsort_ref[...], jnp.concatenate(rows, axis=0)))


def unpack_kernel(in_ref, unpack_ref, first_ref, out_ref):
    steps, columns, states = out_ref.shape
    width = columns // in_ref.shape[1]
    for third in range(in_ref.shape[1]):
        rows = mul(unpack_ref[...], rows_of(in_ref, third)).astype(jnp.bfloat16)
        rows = rows.reshape(steps, width, states)
        out_ref[:, third * width : (third + 1) * width] = rows
        first_ref[third * width : (third + 1) * width] = rows[0]


def update_kernel(last, correction_ref, before_ref, next_ref, residual_ref, jacobians_ref,
                  pack_ref, out_ref, extra_ref, held, sem):
    steps, columns, states = correction_ref.shape
    copies = [
        pltpu.make_async_copy(jacobians_ref.at[step], held.at[step], sem.at[step])
        for step in range(steps)
    ]
    for copy in copies:
        copy.start()
    for step in range(steps):
        correction = correction_ref[step].astype(jnp.float32)
        if last:
            extra_ref[step] = before_ref[step].astype(jnp.float32) + correction
        following = correction_ref[step + 1] if step + 1 < steps else next_ref[...]
        copies[step].wait()
        carried = mul(following, held[step])
        out_ref[step] = residual_ref[step] - (correction - carried)
    if not last:
        thirds = extra_ref.shape[1]
        width = columns // thirds
        for third in range(thirds):
            rows = out_ref[:, third * width : (third + 1) * width].astype(jnp.bfloat16)
            put_rows(extra_ref, third, mul(pack_ref[...], rows.reshape(steps * width, states)))


def vmem():
    return pl.BlockSpec(memory_space=pltpu.VMEM)


def call(kernel, out_shape, args, limit, scratch=(), hbm=(), flops=1 << 28, **kwargs):
    return pl.pallas_call(
        kernel,
        out_shape=out_shape,
        in_specs=[
            pl.BlockSpec(memory_space=pl.ANY) if i in hbm else vmem() for i in range(len(args))
        ],
        out_specs=jax.tree.map(lambda _: vmem(), out_shape),
        scratch_shapes=list(scratch),
        compiler_params=pltpu.CompilerParams(vmem_limit_bytes=limit * MIB),
        cost_estimate=pl.CostEstimate(flops=flops, bytes_accessed=4 * MIB, transcendentals=0),
        **kwargs,
    )(*args)


def exchange(block):
    return lax.all_to_all(block, "tm", split_axis=0, concat_axis=0, tiled=True)


def body(objective, jacobians, precond_blocks):
    local_steps, columns, states = objective.shape
    groups = lax.axis_size("tm")
    steps = local_steps * groups
    thirds = columns // (2 * groups)
    width = columns // thirds
    forward, backward = (jnp.asarray(split_table(t)) for t in tables(steps, groups))
    pack, sort = shuffles(groups)
    unpack, unsort = jnp.asarray(pack.T.copy()), jnp.asarray(sort.T.copy())
    pack, sort = jnp.asarray(pack), jnp.asarray(sort)
    route = [(i + 1, i) for i in range(groups - 1)]
    wire = jax.ShapeDtypeStruct((groups, thirds, 8, states), jnp.bfloat16)
    field = jax.ShapeDtypeStruct(objective.shape, jnp.float32)
    plain = jax.ShapeDtypeStruct(objective.shape, jnp.bfloat16)
    row = jax.ShapeDtypeStruct((columns, states), jnp.bfloat16)

    send = pl.pallas_call(
        pack_kernel,
        grid=(thirds,),
        out_shape=wire,
        in_specs=[
            pl.BlockSpec((local_steps, width, states), lambda i: (0, i, 0)),
            pl.BlockSpec((2 * steps, 2 * steps), lambda i: (0, 0)),
        ],
        out_specs=pl.BlockSpec((groups, 1, 8, states), lambda i: (0, i, 0, 0)),
        compiler_params=pltpu.CompilerParams(vmem_limit_bytes=16 * MIB),
    )(objective, pack)
    residual = objective
    before = None
    for iteration in range(ITERS):
        last = iteration == ITERS - 1
        rows = call(transform_kernel, wire, (exchange(send), forward), 16)
        rows = call(
            multiply_kernel,
            wire,
            (exchange(rows), sort, unsort, precond_blocks),
            32,
            scratch=[
                pltpu.VMEM((3, 2, states, states), jnp.bfloat16),
                pltpu.VMEM((4 * columns, states), jnp.bfloat16),
                pltpu.SemaphoreType.DMA((3, 2)),
            ],
            hbm=(3,),
            flops=1 << 31,
        )
        rows = call(transform_kernel, wire, (exchange(rows), backward), 16)
        first, correction = call(unpack_kernel, (row, plain), (exchange(rows), unpack), 16)
        following = lax.ppermute(first, "tm", route)
        before = correction if before is None else before
        residual, send = call(
            functools.partial(update_kernel, last),
            (field, field if last else wire),
            (correction, before, following, residual, jacobians, pack),
            32,
            scratch=[
                pltpu.VMEM((local_steps, states, states), jnp.bfloat16),
                pltpu.SemaphoreType.DMA((local_steps,)),
            ],
            hbm=(4,),
            flops=1 << 30,
        )
    return (send, residual)


def solution(mesh):
    in_specs = (P("tm", "obj", None), P("tm", None, None), P(None, "tm", None, None))
    out_specs = (P("tm", "obj", None), P("tm", "obj", None))
    return jax.shard_map(body, mesh=mesh, in_specs=in_specs, out_specs=out_specs, check_vma=False)
```

time: 332 us -> 233 us (0.70)
  matrix products: 60.6 us -> 0 us
  local copies, waits for them, and re-layouts: 60.2 us -> 3.56 us
  Pallas kernels: 0 us -> 25.6 us
  other arithmetic: 7.71 us -> 0.01 us
    dot_general x34 -> x0, matrix products: 60.6 us -> none  [the longest x24 47.2 us: mul(): return jnp.dot(left, right, preferred_element_type=jnp.float32)]
    pallas_call x0 -> x11, Pallas kernels: none -> 25.6 us  [the longest x10 24.6 us: call(): pl.pallas_call(kernel, out_shape=out_shape, in_specs=[pl.BlockSpec(memory...]
    another operation x20 -> x0, local copies, waits for them, and re-layouts: 18.7 us -> none  [the longest x8 6.95 us: body(): wave += [jnp.stack(part).reshape(shape) for part in other]]
    reshape x12 -> x0, local copies, waits for them, and re-layouts: 16.7 us -> none  [the longest x2 6.01 us: body(): spectrum.reshape(2, groups, 4, third, states).transpose(1, 0, 3, 2, 4)]
    transpose x9 -> x0, local copies, waits for them, and re-layouts: 10.2 us -> none  [the longest x2 3.04 us: body(): wave = jnp.concatenate(wave, axis=0).transpose(2, 1, 3, 0, 4)]
    convert_element_type x3 -> x0, local copies, waits for them, and re-layouts: 5.47 us -> none  [the longest x2 3.1 us: body(): values.astype(jnp.bfloat16).reshape(2, groups, local_steps, third, states)]
    transpose x3 -> x0, other arithmetic: 4.3 us -> none  [the longest x2 4.18 us: body(): wave = jnp.concatenate(wave, axis=0).transpose(2, 1, 3, 0, 4)]
  transfers between devices with their start and end apart: 2 -> 2, of which waited for: 2 -> 2; matrix products, arithmetic and copies ran while one was open for 1% -> 0% of each run, Pallas kernels for 0% -> 0%
where the time goes in v1:
time: 233 us
  blocking collectives  187 us (80%)
  Pallas kernels  25.6 us (11%)
  waiting for transfers between devices  11.4 us (5%)
  starting transfers between devices  4.63 us (2%)
  local copies, waits for them, and re-layouts  3.56 us (2%)
    all_to_all x8, blocking collectives, exchange(): return lax.all_to_all(block, 'tm', split_axis=0, concat_axis=0, tiled=True)  187 us
    pallas_call x10, Pallas kernels, call(): pl.pallas_call(kernel, out_shape=out_shape, in_specs=[pl.BlockSpec(memory...  24.6 us
    ppermute x2, waiting for transfers between devices, body(): following = lax.ppermute(first, 'tm', route)  11.4 us
  transfers between devices with their start and end apart: 2, of which 2 were waited for; matrix products, arithmetic and copies ran while one was open for 0% of the time, Pallas kernels for 0%

profile of v1, /device:TPU:1, one launch (start us, length us, event | category | flops | bytes accessed | tf_op | source)
XLA Modules:
  0.0 232.9 jit_solution(5479895249439808774)
XLA Ops:
  0.6 0.0 copy-start.1
  0.6 1.7 copy-done.1
  2.3 0.9 copy-done.3
  3.2 1.1 shard_map.104
  4.3 27.5 %all_to_all.40.in_ref = bf16[32,3,8,768]{3,2,1,0:T(8,128)(2,1)S(1)} all-to-all(bf16[32,3,8,768]{3,2,1,0:T(8,128)(2,1)S(1)} %shard_map.104), channel_id=1, replica_groups=mesh['tm'=32,'obj'=4] {'tm'}, dimensions={0} | all-to-all | bytes 2359296 | tf_op jit(solution)/shard_map/all_to_all | solution.py:196
  31.7 0.9 copy-done.7
  32.7 0.8 shard_map.105
  33.5 0.0 slice-start
  33.5 22.7 %all_to_all.41.in_ref = bf16[32,3,8,768]{3,2,1,0:T(8,128)(2,1)S(1)} all-to-all(bf16[32,3,8,768]{3,2,1,0:T(8,128)(2,1)S(1)} %shard_map.105), channel_id=1, replica_groups=mesh['tm'=32,'obj'=4] {'tm'}, dimensions={0} | all-to-all | bytes 2359296 | tf_op jit(solution)/shard_map/all_to_all | solution.py:196
  56.3 0.0 slice-start.1
  56.3 6.1 %shard_map.106 = bf16[32,3,8,768]{3,2,1,0:T(8,128)(2,1)S(1)} custom-call(bf16[32,3,8,768]{3,2,1,0:T(8,128)(2,1)S(1)} %all_to_all.41.in_ref, bf16[256,256]{1,0:T(8,128)(2,1)S(1)} %copy-done.5, bf16[256,256]{1,0:T(8,128)(2,1)S(1)} %copy-done.4, bf16[2,4,768,768]{3,2,1,0:T(8,128)(2,1)S(1)} %copy-done), custom_call_target="tpu_custom_call" | custom-call | flops 2147483648 | bytes 4194304 | tf_op jit(solution)/shard_map/pallas_call | solution.py:181
  62.4 0.0 copy-start.6
  62.4 22.6 %all_to_all.42.in_ref = bf16[32,3,8,768]{3,2,1,0:T(8,128)(2,1)S(1)} all-to-all(bf16[32,3,8,768]{3,2,1,0:T(8,128)(2,1)S(1)} %shard_map.106), channel_id=1, replica_groups=mesh['tm'=32,'obj'=4] {'tm'}, dimensions={0} | all-to-all | bytes 2359296 | tf_op jit(solution)/shard_map/all_to_all | solution.py:196
  85.0 0.8 shard_map.107
  85.8 0.0 copy-start.2
  85.8 22.6 %all_to_all.43.in_ref = bf16[32,3,8,768]{3,2,1,0:T(8,128)(2,1)S(1)} all-to-all(bf16[32,3,8,768]{3,2,1,0:T(8,128)(2,1)S(1)} %shard_map.107), channel_id=1, replica_groups=mesh['tm'=32,'obj'=4] {'tm'}, dimensions={0} | all-to-all | bytes 2359296 | tf_op jit(solution)/shard_map/all_to_all | solution.py:196
  108.4 0.5 shard_map.108
  108.9 2.3 collective-permute-start
  111.2 5.7 %collective-permute-done.next_ref = bf16[192,768]{1,0:T(8,128)(2,1)S(1)} collective-permute-done((bf16[192,768]{1,0:T(8,128)(2,1)S(1)}, bf16[192,768]{1,0:T(8,128)(2,1)S(1)}, u32[]{:S(2)}, u32[]{:S(2)}) %collective-permute-start) | collective-permute-done | bytes 294944 | tf_op jit(solution)/shard_map/ppermute | solution.py:246
  117.0 3.4 %shard_map.109 = (f32[4,192,768]{2,1,0:T(8,128)S(1)}, bf16[32,3,8,768]{3,2,1,0:T(8,128)(2,1)S(1)}) custom-call(bf16[4,192,768]{2,1,0:T(8,128)(2,1)S(1)} %get-tuple-element.10.correction_ref.before_ref, bf16[4,192,768]{2,1,0:T(8,128)(2,1)S(1)} %get-tuple-element.10.correction_ref.before_ref, bf16[192,768]{1,0:T(8,128)(2,1)S(1)} %collective-permute-done.next_ref, ...), custom_call_target="tpu_custom_call" | custom-call | flops 1073741824 | bytes 4194304 | tf_op jit(solution)/shard_map/pallas_call | solution.py:181
  120.4 0.0 copy-start.8
  120.4 23.8 %all_to_all.44.in_ref = bf16[32,3,8,768]{3,2,1,0:T(8,128)(2,1)S(1)} all-to-all(bf16[32,3,8,768]{3,2,1,0:T(8,128)(2,1)S(1)} %get-tuple-element.12), channel_id=1, replica_groups=mesh['tm'=32,'obj'=4] {'tm'}, dimensions={0} | all-to-all | bytes 2359296 | tf_op jit(solution)/shard_map/all_to_all | solution.py:196
  144.2 0.8 shard_map.110
  144.9 22.5 %all_to_all.45.in_ref = bf16[32,3,8,768]{3,2,1,0:T(8,128)(2,1)S(1)} all-to-all(bf16[32,3,8,768]{3,2,1,0:T(8,128)(2,1)S(1)} %shard_map.110), channel_id=1, replica_groups=mesh['tm'=32,'obj'=4] {'tm'}, dimensions={0} | all-to-all | bytes 2359296 | tf_op jit(solution)/shard_map/all_to_all | solution.py:196
  167.4 6.1 %shard_map.111 = bf16[32,3,8,768]{3,2,1,0:T(8,128)(2,1)S(1)} custom-call(bf16[32,3,8,768]{3,2,1,0:T(8,128)(2,1)S(1)} %all_to_all.45.in_ref, bf16[256,256]{1,0:T(8,128)(2,1)S(1)} %copy-done.5, bf16[256,256]{1,0:T(8,128)(2,1)S(1)} %copy-done.4, bf16[2,4,768,768]{3,2,1,0:T(8,128)(2,1)S(1)} %copy-done), custom_call_target="tpu_custom_call" | custom-call | flops 2147483648 | bytes 4194304 | tf_op jit(solution)/shard_map/pallas_call | solution.py:181
  173.5 22.5 %all_to_all.46.in_ref = bf16[32,3,8,768]{3,2,1,0:T(8,128)(2,1)S(1)} all-to-all(bf16[32,3,8,768]{3,2,1,0:T(8,128)(2,1)S(1)} %shard_map.111), channel_id=1, replica_groups=mesh['tm'=32,'obj'=4] {'tm'}, dimensions={0} | all-to-all | bytes 2359296 | tf_op jit(solution)/shard_map/all_to_all | solution.py:196
  196.0 0.8 shard_map.112
  196.8 22.5 %all_to_all.47.in_ref = bf16[32,3,8,768]{3,2,1,0:T(8,128)(2,1)S(1)} all-to-all(bf16[32,3,8,768]{3,2,1,0:T(8,128)(2,1)S(1)} %shard_map.112), channel_id=1, replica_groups=mesh['tm'=32,'obj'=4] {'tm'}, dimensions={0} | all-to-all | bytes 2359296 | tf_op jit(solution)/shard_map/all_to_all | solution.py:196
  219.3 0.5 shard_map.113
  219.7 2.3 collective-permute-start.1
  222.1 5.7 %collective-permute-done.1.next_ref = bf16[192,768]{1,0:T(8,128)(2,1)S(1)} collective-permute-done((bf16[192,768]{1,0:T(8,128)(2,1)S(1)}, bf16[192,768]{1,0:T(8,128)(2,1)S(1)}, u32[]{:S(2)}, u32[]{:S(2)}) %collective-permute-start.1) | collective-permute-done | bytes 294944 | tf_op jit(solution)/shard_map/ppermute | solution.py:246
  227.8 4.9 %shard_map.114 = (f32[4,192,768]{2,1,0:T(8,128)}, f32[4,192,768]{2,1,0:T(8,128)}) custom-call(bf16[4,192,768]{2,1,0:T(8,128)(2,1)S(1)} %get-tuple-element.13.correction_ref, bf16[4,192,768]{2,1,0:T(8,128)(2,1)S(1)} %get-tuple-element.10.correction_ref.before_ref, bf16[192,768]{1,0:T(8,128)(2,1)S(1)} %collective-permute-done.1.next_ref, ...), custom_call_target="tpu_custom_call" | custom-call | flops 1073741824 | bytes 4194304 | tf_op jit(solution)/shard_map/pallas_call | solution.py:181
  (14 shorter events, 0.0 us)
Async XLA Ops:
  0.6 1.7 copy-start.1
  2.3 0.9 copy-start.3
  3.2 53.0 %copy-start = (bf16[2,4,768,768]{3,2,1,0:T(8,128)(2,1)S(1)}, bf16[2,4,768,768]{3,2,1,0:T(8,128)(2,1)}, u32[]{:S(2)}) copy-start(bf16[2,4,768,768]{3,2,1,0:T(8,128)(2,1)} %blocks_ref.3) | copy-start | bytes 28311556
  31.7 1.0 copy-start.7
  32.7 23.6 %copy-start.4 = (bf16[256,256]{1,0:T(8,128)(2,1)S(1)}, bf16[256,256]{1,0:T(8,128)(2,1)}, u32[]{:S(2)}) copy-start(bf16[256,256]{1,0:T(8,128)(2,1)} %constant.11.clone.pack_ref.unsort_ref) | copy-start | bytes 393220
  32.7 23.6 %copy-start.5 = (bf16[256,256]{1,0:T(8,128)(2,1)S(1)}, bf16[256,256]{1,0:T(8,128)(2,1)}, u32[]{:S(2)}) copy-start(bf16[256,256]{1,0:T(8,128)(2,1)} %constant.10.clone.sort_ref.unpack_ref) | copy-start | bytes 393220
  33.5 83.5 %slice-start = ((s8[4718592]{0:T(1024)(128)(4,1)}), s8[4194304]{0:T(1024)(128)(4,1)S(1)}, s32[]{:S(2)}) async-start(s8[4718592]{0:T(1024)(128)(4,1)} %bitcast), calls=%async_computation.8 | async-start | bytes 8388608
  56.3 60.7 %slice-start.1 = ((s8[4718592]{0:T(1024)(128)(4,1)}), s8[524288]{0:T(1024)(128)(4,1)S(1)}, s32[]{:S(2)}) async-start(s8[4718592]{0:T(1024)(128)(4,1)} %bitcast), calls=%async_computation.9 | async-start | bytes 1048576
  62.4 22.6 %copy-start.6 = (bf16[256,512]{1,0:T(8,128)(2,1)S(1)}, bf16[256,512]{1,0:T(8,128)(2,1)}, u32[]{:S(2)}) copy-start(bf16[256,512]{1,0:T(8,128)(2,1)} %constant.9.clone.table_ref) | copy-start | bytes 786436
  85.8 31.2 %copy-start.2 = (f32[4,192,768]{2,1,0:T(8,128)S(1)}, f32[4,192,768]{2,1,0:T(8,128)}, u32[]{:S(2)}) copy-start(f32[4,192,768]{2,1,0:T(8,128)} %residual_ref.1) | copy-start | bytes 7077892
  108.9 8.0 %collective-permute-start = (bf16[192,768]{1,0:T(8,128)(2,1)S(1)}, bf16[192,768]{1,0:T(8,128)(2,1)S(1)}, u32[]{:S(2)}, u32[]{:S(2)}) collective-permute-start(bf16[192,768]{1,0:T(8,128)(2,1)S(1)} %get-tuple-element.11), channel_id=1, source_target_pairs={{4,0},{8,4},{12,8},{16,12},{20,16},{24,20},{28,24},{32,28},{36,32}... | collective-permute-start | bytes 884744 | tf_op jit(solution)/shard_map/ppermute | solution.py:246
  120.4 23.8 %copy-start.8 = (bf16[256,512]{1,0:T(8,128)(2,1)S(1)}, bf16[256,512]{1,0:T(8,128)(2,1)}, u32[]{:S(2)}) copy-start(bf16[256,512]{1,0:T(8,128)(2,1)} %constant.8.clone.table_ref) | copy-start | bytes 786436
  219.7 8.0 %collective-permute-start.1 = (bf16[192,768]{1,0:T(8,128)(2,1)S(1)}, bf16[192,768]{1,0:T(8,128)(2,1)S(1)}, u32[]{:S(2)}, u32[]{:S(2)}) collective-permute-start(bf16[192,768]{1,0:T(8,128)(2,1)S(1)} %get-tuple-element.14), channel_id=1, source_target_pairs={{4,0},{8,4},{12,8},{16,12},{20,16},{24,20},{28,24},{32,28},{36,32}... | collective-permute-start | bytes 884744 | tf_op jit(solution)/shard_map/ppermute | solution.py:246

commit v2 on v1

v2 whole, which is shorter than its diff:
```python
import math

import jax
import jax.numpy as jnp
import numpy as np
from jax import lax
from jax.experimental import pallas as pl
from jax.experimental.pallas import tpu as pltpu
from jax.sharding import PartitionSpec as P

log_alpha = math.log(0.05)
MIB = 1 << 20
PACK_LIMIT = 16
PRODUCT_LIMIT = 16


def split_table(table):
    high = table.astype(jnp.bfloat16)
    low = (table - high.astype(np.float64)).astype(jnp.bfloat16)
    return np.concatenate([high, low], axis=1)


def tables(steps, groups):
    local = steps // groups
    times = np.arange(steps)
    forward = np.zeros((groups, 2, 4, 2, steps))
    backward = np.zeros((2, steps, groups, 2, 4))
    grow = np.exp(times * (-log_alpha / steps))
    shrink = np.exp(times * (log_alpha / steps)) / steps
    for group in range(groups):
        low_side = group < groups // 2
        for position in range(2):
            first = (0 if low_side else 1) ^ position
            jobs = [(0, 4 * group + 1, position), (2, 4 * group + 2 * position, first)]
            for slot, frequency, half in jobs:
                angle = 2.0 * math.pi * ((frequency * times) % steps) / steps
                cosine, sine = np.cos(angle), np.sin(angle)
                if frequency % (steps // 2) == 0:
                    for at, part in ((slot, half), (slot + 1, 1 - half)):
                        forward[group, position, at, part] = cosine * grow
                        backward[part, :, group, position, at] = cosine * shrink
                    continue
                forward[group, position, slot, half] = cosine * grow
                forward[group, position, slot + 1, half] = -sine * grow
                backward[half, :, group, position, slot] = 2.0 * cosine * shrink
                backward[half, :, group, position, slot + 1] = -2.0 * sine * shrink
    size = 2 * steps
    forward = forward.reshape(size, 2, steps)
    backward = backward.reshape(2, steps, size)

    def by_owner(shift):
        ahead = np.roll(forward, -shift, axis=2).reshape(size, 2, groups, local)
        back = np.roll(backward, -shift, axis=1).reshape(2, groups, local, size)
        ahead = ahead.transpose(0, 2, 1, 3).reshape(size, size)
        return ahead, back.transpose(1, 0, 2, 3).reshape(size, size)

    beyond = np.concatenate([backward[:, local::local], np.zeros((2, 1, size))], axis=1)
    return (*by_owner(0), *by_owner(1), beyond.reshape(2 * groups, size))


def shuffles(groups):
    size = 8 * groups
    pack = np.zeros((groups, 2, 4, 4, 2, groups))
    sort = np.zeros((4, 2, groups, groups, 2, 4))
    for piece in range(groups):
        for half in range(2):
            for step in range(4):
                pack[piece, half, step, step, half, piece] = 1
                sort[step, half, piece, piece, half, step] = 1
    shape = (size, size)
    return pack.reshape(shape).astype(jnp.bfloat16), sort.reshape(shape).astype(jnp.bfloat16)


def mul(left, right):
    return jnp.dot(left, right, preferred_element_type=jnp.float32)


def rows_of(ref, third):
    groups, _, eight, states = ref.shape
    wide = ref[:, third].astype(jnp.float32)
    return wide.reshape(groups * eight, states).astype(jnp.bfloat16)


def put_rows(ref, third, rows):
    groups, _, eight, states = ref.shape
    ref[:, third] = rows.reshape(groups, eight, states).astype(ref.dtype)


def pack_kernel(block_ref, pack_ref, table_ref, send_ref, kept_ref):
    steps, columns, states = block_ref.shape
    rows = block_ref[...].reshape(steps * columns, states).astype(jnp.bfloat16)
    put_rows(send_ref, 0, mul(pack_ref[...], rows))

    @pl.when(pl.program_id(0) == 0)
    def _():
        kept_ref[...] = table_ref[...]


def transform_kernel(*refs):
    *in_refs, table_ref, out_ref = refs
    for third in range(out_ref.shape[1]):
        rows = []
        for in_ref in in_refs:
            rows += [rows_of(in_ref, third)] * 2
        put_rows(out_ref, third, mul(table_ref[...], jnp.concatenate(rows, axis=0)))


def last_transform_kernel(before_ref, in_ref, table_ref, beyond_ref, spread_ref, out_ref):
    groups, thirds = in_ref.shape[:2]
    extra = []
    for third in range(thirds):
        rows = rows_of(in_ref, third)
        rows = jnp.concatenate([rows, rows], axis=0)
        extra.append(mul(beyond_ref[...], rows).astype(jnp.bfloat16))
        before = rows_of(before_ref, third)
        rows = jnp.concatenate([before, before, rows], axis=0)
        put_rows(out_ref, third, mul(table_ref[...], rows))
    extra.append(jnp.zeros_like(extra[0]))
    put_rows(out_ref, thirds, mul(spread_ref[...], jnp.concatenate(extra, axis=0)))


def multiply_kernel(in_ref, sort_ref, unsort_ref, blocks_ref, out_ref, sorted_ref):
    groups, thirds, _, states = in_ref.shape
    half = thirds * groups
    for third in range(thirds):
        rows = mul(sort_ref[...], rows_of(in_ref, third)).astype(jnp.bfloat16)
        for block in range(8):
            at = block * half + third * groups
            sorted_ref[at : at + groups] = rows[block * groups : (block + 1) * groups]

    def product(frequency, re_at, im_at, count):
        left = jnp.concatenate(
            [sorted_ref[re_at : re_at + count], sorted_ref[im_at : im_at + count]], axis=0
        )
        y = mul(left, blocks_ref[0, frequency])
        z = mul(left, blocks_ref[1, frequency])
        sorted_ref[re_at : re_at + count] = (y[:count] - z[count:]).astype(jnp.bfloat16)
        sorted_ref[im_at : im_at + count] = (z[:count] + y[count:]).astype(jnp.bfloat16)

    product(1, 0, 2 * half, 2 * half)
    product(0, 4 * half, 6 * half, half)
    product(2, 5 * half, 7 * half, half)
    for third in range(thirds):
        at = third * groups
        rows = [sorted_ref[block * half + at : block * half + at + groups] for block in range(8)]
        put_rows(out_ref, third, mul(unsort_ref[...], jnp.concatenate(rows, axis=0)))


def carry_kernel(in_ref, residual_ref, jacobians_ref, pack_ref, unpack_ref,
                 following_ref, held_ref, send_ref):
    steps, columns, states = held_ref.shape
    thirds = in_ref.shape[1]
    width = columns // thirds
    for third in range(thirds):
        rows = mul(unpack_ref[...], rows_of(in_ref, third)).astype(jnp.bfloat16)
        following_ref[:, third * width : (third + 1) * width] = rows.reshape(steps, width, states)
    at_end = lax.axis_index("tm") == in_ref.shape[0] - 1
    for step in range(steps):
        carried = mul(following_ref[step], jacobians_ref[step])
        if step == steps - 1:
            carried = jnp.where(at_end, 0.0, 1.0) * carried
        held_ref[step] = residual_ref[step] + carried
    for third in range(thirds):
        rows = held_ref[:, third * width : (third + 1) * width].astype(jnp.bfloat16)
        put_rows(send_ref, third, mul(pack_ref[...], rows.reshape(steps * width, states)))


def finish_kernel(in_ref, following_ref, held_ref, jacobians_ref, unpack_ref, sort_ref,
                  adjoint_hbm, residual_hbm, adjoint_ref, residual_ref, sem):
    steps, columns, states = held_ref.shape
    thirds = in_ref.shape[1] - 1
    width = columns // thirds
    for third in range(thirds):
        rows = mul(unpack_ref[...], rows_of(in_ref, third))
        adjoint_ref[:, third * width : (third + 1) * width] = rows.reshape(steps, width, states)
    copies = []

    def put(index, source, target, step):
        copy = pltpu.make_async_copy(source.at[step], target.at[step], sem.at[index, step])
        copy.start()
        copies.append(copy)

    for step in range(steps):
        put(0, adjoint_ref, adjoint_hbm, step)
    for step in range(steps):
        if step + 1 < steps:
            following = adjoint_ref[step + 1] - following_ref[step].astype(jnp.float32)
            following = following.astype(jnp.bfloat16)
        else:
            following = mul(sort_ref[...], rows_of(in_ref, thirds))[:columns]
            following = following.astype(jnp.bfloat16)
        carried = mul(following, jacobians_ref[step])
        residual_ref[step] = held_ref[step] - (adjoint_ref[step] - carried)
        put(1, residual_ref, residual_hbm, step)
    for copy in copies:
        copy.wait()


def vmem():
    return pl.BlockSpec(memory_space=pltpu.VMEM)


def call(kernel, out_shape, args, limit, scratch=(), out_space=pltpu.VMEM, flops=1 << 28):
    return pl.pallas_call(
        kernel,
        out_shape=out_shape,
        in_specs=[vmem()] * len(args),
        out_specs=jax.tree.map(lambda _: pl.BlockSpec(memory_space=out_space), out_shape),
        scratch_shapes=list(scratch),
        compiler_params=pltpu.CompilerParams(vmem_limit_bytes=limit * MIB),
        cost_estimate=pl.CostEstimate(flops=flops, bytes_accessed=4 * MIB, transcendentals=0),
    )(*args)


def exchange(block):
    return lax.all_to_all(block, "tm", split_axis=0, concat_axis=0, tiled=True)


def body(objective, jacobians, precond_blocks):
    local_steps, columns, states = objective.shape
    groups = lax.axis_size("tm")
    steps = local_steps * groups
    thirds = columns // (2 * groups)
    width = columns // thirds
    forward, backward, forward_next, backward_next, beyond = tables(steps, groups)
    forward, backward, subtract_next, backward_next, beyond = (
        split_table(t) for t in (forward, backward, -forward_next, backward_next, beyond)
    )
    second = np.concatenate([forward, subtract_next], axis=1)
    both = np.concatenate([backward, backward], axis=1)
    pack, sort = shuffles(groups)
    unpack, unsort = pack.T.copy(), sort.T.copy()
    forward, second, both, backward_next, beyond, pack, unpack, sort, unsort = (
        jnp.asarray(t)
        for t in (forward, second, both, backward_next, beyond, pack, unpack, sort, unsort)
    )
    wire = jax.ShapeDtypeStruct((groups, thirds, 8, states), jnp.bfloat16)
    longer = jax.ShapeDtypeStruct((groups, thirds + 1, 8, states), jnp.bfloat16)
    field = jax.ShapeDtypeStruct(objective.shape, jnp.float32)
    plain = jax.ShapeDtypeStruct(objective.shape, jnp.bfloat16)

    def multiply(rows):
        return call(
            multiply_kernel,
            wire,
            (rows, sort, unsort, precond_blocks),
            PRODUCT_LIMIT,
            scratch=[pltpu.VMEM((4 * columns, states), jnp.bfloat16)],
            flops=1 << 31,
        )

    whole = lambda i: (0, 0)
    send, table = pl.pallas_call(
        pack_kernel,
        grid=(thirds,),
        out_shape=(wire, jax.ShapeDtypeStruct(forward.shape, forward.dtype)),
        in_specs=[
            pl.BlockSpec((local_steps, width, states), lambda i: (0, i, 0)),
            pl.BlockSpec(pack.shape, whole),
            pl.BlockSpec(forward.shape, whole),
        ],
        out_specs=(
            pl.BlockSpec((groups, 1, 8, states), lambda i: (0, i, 0, 0)),
            pl.BlockSpec(forward.shape, whole),
        ),
        compiler_params=pltpu.CompilerParams(vmem_limit_bytes=PACK_LIMIT * MIB),
    )(objective, pack, forward)
    rows = call(transform_kernel, wire, (exchange(send), table), 16)
    wave = exchange(multiply(exchange(rows)))
    ahead = call(transform_kernel, wire, (wave, backward_next), 16)
    following, held, send = call(
        carry_kernel,
        (plain, field, wire),
        (exchange(ahead), objective, jacobians, pack, unpack),
        16,
        flops=1 << 30,
    )
    rows = call(transform_kernel, wire, (exchange(send), ahead, second), 16)
    again = exchange(multiply(exchange(rows)))
    rows = call(last_transform_kernel, longer, (wave, again, both, beyond, unsort), 16)
    return call(
        finish_kernel,
        (field, field),
        (exchange(rows), following, held, jacobians, unpack, sort),
        16,
        scratch=[
            pltpu.VMEM(objective.shape, jnp.float32),
            pltpu.VMEM(objective.shape, jnp.float32),
            pltpu.SemaphoreType.DMA((2, local_steps)),
        ],
        out_space=pl.ANY,
        flops=1 << 30,
    )


def solution(mesh):
    in_specs = (P("tm", "obj", None), P("tm", None, None), P(None, "tm", None, None))
    out_specs = (P("tm", "obj", None), P("tm", "obj", None))
    return jax.shard_map(body, mesh=mesh, in_specs=in_specs, out_specs=out_specs, check_vma=False)
```

time: 233 us -> 211 us (0.906)
  waiting for transfers between devices: 11.4 us -> 0 us
  Pallas kernels: 25.6 us -> 16.9 us
  starting transfers between devices: 4.63 us -> 0 us
    ppermute x2 -> x0, waiting for transfers between devices: 11.4 us -> none  [body(): following = lax.ppermute(first, 'tm', route)]
    pallas_call x11 -> x9, Pallas kernels: 25.6 us -> 16.9 us  [the longest x8 15.8 us: call(): pl.pallas_call(kernel, out_shape=out_shape, in_specs=[vmem()] * len(args)...]
    ppermute x2 -> x0, starting transfers between devices: 4.63 us -> none  [body(): following = lax.ppermute(first, 'tm', route)]
    all_to_all x8, blocking collectives: 187 us -> 189 us  [exchange(): return lax.all_to_all(block, 'tm', split_axis=0, concat_axis=0, tiled=True)]
  transfers between devices with their start and end apart: 2 -> 0, of which waited for: 2 -> 0; matrix products, arithmetic and copies ran while one was open for 0% -> 0% of each run, Pallas kernels for 0% -> 0%
where the time goes in v2:
time: 211 us
  blocking collectives  189 us (90%)
  Pallas kernels  16.9 us (8%)
  local copies, waits for them, and re-layouts  3.57 us (2%)
    all_to_all x8, blocking collectives, exchange(): return lax.all_to_all(block, 'tm', split_axis=0, concat_axis=0, tiled=True)  189 us
    pallas_call x8, Pallas kernels, call(): pl.pallas_call(kernel, out_shape=out_shape, in_specs=[vmem()] * len(args)...  15.8 us

profile of v2, /device:TPU:1, one launch (start us, length us, event | category | flops | bytes accessed | tf_op | source)
XLA Modules:
  0.0 210.9 jit_solution(2503731046692142773)
XLA Ops:
  0.6 0.0 copy-start.1
  0.6 1.7 copy-done.1
  2.3 0.9 copy-done.4
  3.2 0.9 copy-done.9
  4.2 1.1 shard_map.131
  5.3 27.5 %all_to_all.40.refs_0_ = bf16[32,3,8,768]{3,2,1,0:T(8,128)(2,1)S(1)} all-to-all(bf16[32,3,8,768]{3,2,1,0:T(8,128)(2,1)S(1)} %get-tuple-element.7), channel_id=1, replica_groups=mesh['tm'=32,'obj'=4] {'tm'}, dimensions={0} | all-to-all | bytes 2359296 | tf_op jit(solution)/shard_map/all_to_all | solution.py:216
  32.8 0.8 shard_map.132
  33.5 0.0 slice-start
  33.6 22.7 %all_to_all.41.in_ref = bf16[32,3,8,768]{3,2,1,0:T(8,128)(2,1)S(1)} all-to-all(bf16[32,3,8,768]{3,2,1,0:T(8,128)(2,1)S(1)} %shard_map.132), channel_id=1, replica_groups=mesh['tm'=32,'obj'=4] {'tm'}, dimensions={0} | all-to-all | bytes 2359296 | tf_op jit(solution)/shard_map/all_to_all | solution.py:216
  56.3 0.0 copy-done
  56.3 0.0 copy-done.5
  56.3 0.0 slice-start.1
  56.3 3.2 %shard_map.133 = bf16[32,3,8,768]{3,2,1,0:T(8,128)(2,1)S(1)} custom-call(bf16[32,3,8,768]{3,2,1,0:T(8,128)(2,1)S(1)} %all_to_all.41.in_ref, bf16[256,256]{1,0:T(8,128)(2,1)S(1)} %copy-done.3, bf16[256,256]{1,0:T(8,128)(2,1)S(1)} %copy-done.5, bf16[2,4,768,768]{3,2,1,0:T(8,128)(2,1)S(1)} %copy-done), custom_call_target="tpu_custom_call" | custom-call | flops 2147483648 | bytes 4194304 | tf_op jit(solution)/shard_map/pallas_call | solution.py:204
  59.5 0.0 copy-start.8
  59.5 22.6 %all_to_all.42.refs_0_.before_ref = bf16[32,3,8,768]{3,2,1,0:T(8,128)(2,1)S(1)} all-to-all(bf16[32,3,8,768]{3,2,1,0:T(8,128)(2,1)S(1)} %shard_map.133), channel_id=1, replica_groups=mesh['tm'=32,'obj'=4] {'tm'}, dimensions={0} | all-to-all | bytes 2359296 | tf_op jit(solution)/shard_map/all_to_all | solution.py:216
  82.2 0.8 shard_map.134.refs_1_
  83.0 0.0 copy-start.2
  83.0 22.6 %all_to_all.43.in_ref = bf16[32,3,8,768]{3,2,1,0:T(8,128)(2,1)S(1)} all-to-all(bf16[32,3,8,768]{3,2,1,0:T(8,128)(2,1)S(1)} %shard_map.134.refs_1_), channel_id=1, replica_groups=mesh['tm'=32,'obj'=4] {'tm'}, dimensions={0} | all-to-all | bytes 2359296 | tf_op jit(solution)/shard_map/all_to_all | solution.py:216
  105.6 0.0 slice-done
  105.6 0.0 copy-done.2
  105.6 1.8 shard_map.135
  107.4 0.0 copy-start.7
  107.4 22.6 %all_to_all.44.refs_0_ = bf16[32,3,8,768]{3,2,1,0:T(8,128)(2,1)S(1)} all-to-all(bf16[32,3,8,768]{3,2,1,0:T(8,128)(2,1)S(1)} %get-tuple-element.9), channel_id=1, replica_groups=mesh['tm'=32,'obj'=4] {'tm'}, dimensions={0} | all-to-all | bytes 2359296 | tf_op jit(solution)/shard_map/all_to_all | solution.py:216
  130.0 1.4 shard_map.136
  131.4 22.5 %all_to_all.45.in_ref = bf16[32,3,8,768]{3,2,1,0:T(8,128)(2,1)S(1)} all-to-all(bf16[32,3,8,768]{3,2,1,0:T(8,128)(2,1)S(1)} %shard_map.136), channel_id=1, replica_groups=mesh['tm'=32,'obj'=4] {'tm'}, dimensions={0} | all-to-all | bytes 2359296 | tf_op jit(solution)/shard_map/all_to_all | solution.py:216
  153.9 3.2 %shard_map.137 = bf16[32,3,8,768]{3,2,1,0:T(8,128)(2,1)S(1)} custom-call(bf16[32,3,8,768]{3,2,1,0:T(8,128)(2,1)S(1)} %all_to_all.45.in_ref, bf16[256,256]{1,0:T(8,128)(2,1)S(1)} %copy-done.3, bf16[256,256]{1,0:T(8,128)(2,1)S(1)} %copy-done.5, bf16[2,4,768,768]{3,2,1,0:T(8,128)(2,1)S(1)} %copy-done), custom_call_target="tpu_custom_call" | custom-call | flops 2147483648 | bytes 4194304 | tf_op jit(solution)/shard_map/pallas_call | solution.py:204
  157.1 0.0 copy-start.6
  157.1 0.0 copy-start.10
  157.1 22.6 %all_to_all.46.in_ref = bf16[32,3,8,768]{3,2,1,0:T(8,128)(2,1)S(1)} all-to-all(bf16[32,3,8,768]{3,2,1,0:T(8,128)(2,1)S(1)} %shard_map.137), channel_id=1, replica_groups=mesh['tm'=32,'obj'=4] {'tm'}, dimensions={0} | all-to-all | bytes 2359296 | tf_op jit(solution)/shard_map/all_to_all | solution.py:216
  179.7 1.9 shard_map.138
  181.7 26.3 %all_to_all.47.in_ref = bf16[32,4,8,768]{3,2,1,0:T(8,128)(2,1)S(1)} all-to-all(bf16[32,4,8,768]{3,2,1,0:T(8,128)(2,1)S(1)} %shard_map.138), channel_id=1, replica_groups=mesh['tm'=32,'obj'=4] {'tm'}, dimensions={0} | all-to-all | bytes 3145728 | tf_op jit(solution)/shard_map/all_to_all | solution.py:216
  207.9 2.8 %shard_map.139 = (f32[4,192,768]{2,1,0:T(8,128)}, f32[4,192,768]{2,1,0:T(8,128)}) custom-call(bf16[32,4,8,768]{3,2,1,0:T(8,128)(2,1)S(1)} %all_to_all.47.in_ref, bf16[4,192,768]{2,1,0:T(8,128)(2,1)S(1)} %get-tuple-element.10.following_ref, f32[4,192,768]{2,1,0:T(8,128)S(1)} %get-tuple-element.11.held_ref, bf16[4,768,768]{2,1,0:T(8,128)(2,1)S(1)} %bitcast.1, ...), custom_call_target="tpu_custom_call" | custom-call | flops 1073741824 | bytes 4194304 | tf_op jit(solution)/shard_map/pallas_call | solution.py:204
  (12 shorter events, 0.0 us)
Async XLA Ops:
  0.6 1.7 copy-start.1
  2.3 0.9 copy-start.4
  3.2 0.9 copy-start.9
  4.2 52.1 %copy-start = (bf16[2,4,768,768]{3,2,1,0:T(8,128)(2,1)S(1)}, bf16[2,4,768,768]{3,2,1,0:T(8,128)(2,1)}, u32[]{:S(2)}) copy-start(bf16[2,4,768,768]{3,2,1,0:T(8,128)(2,1)} %blocks_ref.3) | copy-start | bytes 28311556
  32.7 23.6 %copy-start.3 = (bf16[256,256]{1,0:T(8,128)(2,1)S(1)}, bf16[256,256]{1,0:T(8,128)(2,1)}, u32[]{:S(2)}) copy-start(bf16[256,256]{1,0:T(8,128)(2,1)} %constant.20.clone.sort_ref.unpack_ref) | copy-start | bytes 393220
  32.8 23.6 %copy-start.5 = (bf16[256,256]{1,0:T(8,128)(2,1)S(1)}, bf16[256,256]{1,0:T(8,128)(2,1)}, u32[]{:S(2)}) copy-start(bf16[256,256]{1,0:T(8,128)(2,1)} %constant.19.clone.pack_ref.unsort_ref.spread_ref) | copy-start | bytes 393220
  33.5 72.0 %slice-start = ((s8[4718592]{0:T(1024)(128)(4,1)}), s8[4194304]{0:T(1024)(128)(4,1)S(1)}, s32[]{:S(2)}) async-start(s8[4718592]{0:T(1024)(128)(4,1)} %bitcast), calls=%async_computation.8 | async-start | bytes 8388608
  56.3 49.3 %slice-start.1 = ((s8[4718592]{0:T(1024)(128)(4,1)}), s8[524288]{0:T(1024)(128)(4,1)S(1)}, s32[]{:S(2)}) async-start(s8[4718592]{0:T(1024)(128)(4,1)} %bitcast), calls=%async_computation.9 | async-start | bytes 1048576
  59.5 22.6 %copy-start.8 = (bf16[256,512]{1,0:T(8,128)(2,1)S(1)}, bf16[256,512]{1,0:T(8,128)(2,1)}, u32[]{:S(2)}) copy-start(bf16[256,512]{1,0:T(8,128)(2,1)} %constant.17.clone.refs_1_) | copy-start | bytes 786436
  83.0 22.6 %copy-start.2 = (f32[4,192,768]{2,1,0:T(8,128)S(1)}, f32[4,192,768]{2,1,0:T(8,128)}, u32[]{:S(2)}) copy-start(f32[4,192,768]{2,1,0:T(8,128)} %residual_ref.1) | copy-start | bytes 7077892
  107.4 22.6 %copy-start.7 = (bf16[256,1024]{1,0:T(8,128)(2,1)S(1)}, bf16[256,1024]{1,0:T(8,128)(2,1)}, u32[]{:S(2)}) copy-start(bf16[256,1024]{1,0:T(8,128)(2,1)} %constant.15.clone.refs_2_) | copy-start | bytes 1572868
  157.1 22.6 %copy-start.6 = (bf16[256,1024]{1,0:T(8,128)(2,1)S(1)}, bf16[256,1024]{1,0:T(8,128)(2,1)}, u32[]{:S(2)}) copy-start(bf16[256,1024]{1,0:T(8,128)(2,1)} %constant.16.clone.table_ref) | copy-start | bytes 1572868
  157.1 22.6 %copy-start.10 = (bf16[64,512]{1,0:T(8,128)(2,1)S(1)}, bf16[64,512]{1,0:T(8,128)(2,1)}, u32[]{:S(2)}) copy-start(bf16[64,512]{1,0:T(8,128)(2,1)} %constant.18.clone.beyond_ref) | copy-start | bytes 196612

commit v3 on v2

--- a/solution.py
+++ b/solution.py
@@ -10,8 +10,6 @@
 
 log_alpha = math.log(0.05)
 MIB = 1 << 20
-PACK_LIMIT = 16
-PRODUCT_LIMIT = 16
 
 
 def split_table(table):
@@ -86,14 +84,29 @@
     ref[:, third] = rows.reshape(groups, eight, states).astype(ref.dtype)
 
 
-def pack_kernel(block_ref, pack_ref, table_ref, send_ref, kept_ref):
-    steps, columns, states = block_ref.shape
-    rows = block_ref[...].reshape(steps * columns, states).astype(jnp.bfloat16)
-    put_rows(send_ref, 0, mul(pack_ref[...], rows))
-
-    @pl.when(pl.program_id(0) == 0)
-    def _():
-        kept_ref[...] = table_ref[...]
+def pack_kernel(objective_hbm, table_hbm, send_ref, table_ref, rows_ref, sem):
+    groups, thirds, eight, states = send_ref.shape
+    steps, columns, _ = rows_ref.shape
+    width = columns // thirds
+    copies = []
+    for third in range(thirds):
+        part = pl.ds(third * width, width)
+        copies.append(
+            pltpu.make_async_copy(objective_hbm.at[:, part], rows_ref.at[:, part], sem.at[third])
+        )
+        copies[-1].start()
+    table_copy = pltpu.make_async_copy(table_hbm, table_ref, sem.at[thirds])
+    table_copy.start()
+    shape = (eight * groups, eight * groups)
+    row = lax.broadcasted_iota(jnp.int32, shape, 0)
+    source = (row % steps) * width + (row // steps % 2) * groups + row // eight
+    pack = (source == lax.broadcasted_iota(jnp.int32, shape, 1)).astype(jnp.float32)
+    pack = pack.astype(jnp.bfloat16)
+    for third in range(thirds):
+        copies[third].wait()
+        rows = rows_ref[:, third * width : (third + 1) * width].astype(jnp.bfloat16)
+        put_rows(send_ref, third, mul(pack, rows.reshape(steps * width, states)))
+    table_copy.wait()
 
 
 def transform_kernel(*refs):
@@ -109,11 +122,9 @@
     groups, thirds = in_ref.shape[:2]
     extra = []
     for third in range(thirds):
-        rows = rows_of(in_ref, third)
-        rows = jnp.concatenate([rows, rows], axis=0)
+        before, rows = rows_of(before_ref, third), rows_of(in_ref, third)
+        rows = jnp.concatenate([before, before, rows, rows], axis=0)
         extra.append(mul(beyond_ref[...], rows).astype(jnp.bfloat16))
-        before = rows_of(before_ref, third)
-        rows = jnp.concatenate([before, before, rows], axis=0)
         put_rows(out_ref, third, mul(table_ref[...], rows))
     extra.append(jnp.zeros_like(extra[0]))
     put_rows(out_ref, thirds, mul(spread_ref[...], jnp.concatenate(extra, axis=0)))
@@ -146,9 +157,9 @@
         put_rows(out_ref, third, mul(unsort_ref[...], jnp.concatenate(rows, axis=0)))
 
 
-def carry_kernel(in_ref, residual_ref, jacobians_ref, pack_ref, unpack_ref,
-                 following_ref, held_ref, send_ref):
-    steps, columns, states = held_ref.shape
+def carry_kernel(in_ref, objective_ref, jacobians_ref, pack_ref, unpack_ref, send_ref,
+                 following_ref, sum_ref):
+    steps, columns, states = objective_ref.shape
     thirds = in_ref.shape[1]
     width = columns // thirds
     for third in range(thirds):
@@ -159,52 +170,47 @@
         carried = mul(following_ref[step], jacobians_ref[step])
         if step == steps - 1:
             carried = jnp.where(at_end, 0.0, 1.0) * carried
-        held_ref[step] = residual_ref[step] + carried
-    for third in range(thirds):
-        rows = held_ref[:, third * width : (third + 1) * width].astype(jnp.bfloat16)
+        sum_ref[step] = (objective_ref[step] + carried).astype(jnp.bfloat16)
+    for third in range(thirds):
+        rows = sum_ref[:, third * width : (third + 1) * width]
         put_rows(send_ref, third, mul(pack_ref[...], rows.reshape(steps * width, states)))
 
 
-def finish_kernel(in_ref, following_ref, held_ref, jacobians_ref, unpack_ref, sort_ref,
+def finish_kernel(in_ref, objective_ref, jacobians_ref, unpack_ref, sort_ref,
                   adjoint_hbm, residual_hbm, adjoint_ref, residual_ref, sem):
-    steps, columns, states = held_ref.shape
+    steps, columns, states = objective_ref.shape
     thirds = in_ref.shape[1] - 1
     width = columns // thirds
+    copies = []
+
+    def put(source, target, part, flag):
+        copies.append(pltpu.make_async_copy(source.at[part], target.at[part], flag))
+        copies[-1].start()
+
     for third in range(thirds):
         rows = mul(unpack_ref[...], rows_of(in_ref, third))
         adjoint_ref[:, third * width : (third + 1) * width] = rows.reshape(steps, width, states)
-    copies = []
-
-    def put(index, source, target, step):
-        copy = pltpu.make_async_copy(source.at[step], target.at[step], sem.at[index, step])
-        copy.start()
-        copies.append(copy)
-
-    for step in range(steps):
-        put(0, adjoint_ref, adjoint_hbm, step)
+        part = (slice(None), pl.ds(third * width, width))
+        put(adjoint_ref, adjoint_hbm, part, sem.at[0, third])
     for step in range(steps):
         if step + 1 < steps:
-            following = adjoint_ref[step + 1] - following_ref[step].astype(jnp.float32)
-            following = following.astype(jnp.bfloat16)
+            following = adjoint_ref[step + 1].astype(jnp.bfloat16)
         else:
             following = mul(sort_ref[...], rows_of(in_ref, thirds))[:columns]
             following = following.astype(jnp.bfloat16)
         carried = mul(following, jacobians_ref[step])
-        residual_ref[step] = held_ref[step] - (adjoint_ref[step] - carried)
-        put(1, residual_ref, residual_hbm, step)
+        residual_ref[step] = objective_ref[step] - (adjoint_ref[step] - carried)
+        put(residual_ref, residual_hbm, step, sem.at[1, step])
     for copy in copies:
         copy.wait()
 
 
-def vmem():
-    return pl.BlockSpec(memory_space=pltpu.VMEM)
-
-
-def call(kernel, out_shape, args, limit, scratch=(), out_space=pltpu.VMEM, flops=1 << 28):
+def call(kernel, out_shape, args, limit, scratch=(), in_space=pltpu.VMEM,
+         out_space=pltpu.VMEM, flops=1 << 28):
     return pl.pallas_call(
         kernel,
         out_shape=out_shape,
-        in_specs=[vmem()] * len(args),
+        in_specs=[pl.BlockSpec(memory_space=in_space)] * len(args),
         out_specs=jax.tree.map(lambda _: pl.BlockSpec(memory_space=out_space), out_shape),
         scratch_shapes=list(scratch),
         compiler_params=pltpu.CompilerParams(vmem_limit_bytes=limit * MIB),
@@ -221,13 +227,13 @@
     groups = lax.axis_size("tm")
     steps = local_steps * groups
     thirds = columns // (2 * groups)
-    width = columns // thirds
     forward, backward, forward_next, backward_next, beyond = tables(steps, groups)
     forward, backward, subtract_next, backward_next, beyond = (
         split_table(t) for t in (forward, backward, -forward_next, backward_next, beyond)
     )
     second = np.concatenate([forward, subtract_next], axis=1)
     both = np.concatenate([backward, backward], axis=1)
+    beyond = np.concatenate([beyond, beyond], axis=1)
     pack, sort = shuffles(groups)
     unpack, unsort = pack.T.copy(), sort.T.copy()
     forward, second, both, backward_next, beyond, pack, unpack, sort, unsort = (
@@ -237,42 +243,37 @@
     wire = jax.ShapeDtypeStruct((groups, thirds, 8, states), jnp.bfloat16)
     longer = jax.ShapeDtypeStruct((groups, thirds + 1, 8, states), jnp.bfloat16)
     field = jax.ShapeDtypeStruct(objective.shape, jnp.float32)
-    plain = jax.ShapeDtypeStruct(objective.shape, jnp.bfloat16)
 
     def multiply(rows):
         return call(
             multiply_kernel,
             wire,
             (rows, sort, unsort, precond_blocks),
-            PRODUCT_LIMIT,
+            16,
             scratch=[pltpu.VMEM((4 * columns, states), jnp.bfloat16)],
             flops=1 << 31,
         )
 
-    whole = lambda i: (0, 0)
-    send, table = pl.pallas_call(
+    send, table = call(
         pack_kernel,
-        grid=(thirds,),
-        out_shape=(wire, jax.ShapeDtypeStruct(forward.shape, forward.dtype)),
-        in_specs=[
-            pl.BlockSpec((local_steps, width, states), lambda i: (0, i, 0)),
-            pl.BlockSpec(pack.shape, whole),
-            pl.BlockSpec(forward.shape, whole),
+        (wire, jax.ShapeDtypeStruct(forward.shape, forward.dtype)),
+        (objective, forward),
+        16,
+        scratch=[
+            pltpu.VMEM(objective.shape, jnp.float32),
+            pltpu.SemaphoreType.DMA((thirds + 1,)),
         ],
-        out_specs=(
-            pl.BlockSpec((groups, 1, 8, states), lambda i: (0, i, 0, 0)),
-            pl.BlockSpec(forward.shape, whole),
-        ),
-        compiler_params=pltpu.CompilerParams(vmem_limit_bytes=PACK_LIMIT * MIB),
-    )(objective, pack, forward)
+        in_space=pltpu.HBM,
+    )
     rows = call(transform_kernel, wire, (exchange(send), table), 16)
     wave = exchange(multiply(exchange(rows)))
     ahead = call(transform_kernel, wire, (wave, backward_next), 16)
-    following, held, send = call(
+    send = call(
         carry_kernel,
-        (plain, field, wire),
+        wire,
         (exchange(ahead), objective, jacobians, pack, unpack),
         16,
+        scratch=[pltpu.VMEM(objective.shape, jnp.bfloat16)] * 2,
         flops=1 << 30,
     )
     rows = call(transform_kernel, wire, (exchange(send), ahead, second), 16)
@@ -281,7 +282,7 @@
     return call(
         finish_kernel,
         (field, field),
-        (exchange(rows), following, held, jacobians, unpack, sort),
+        (exchange(rows), objective, jacobians, unpack, sort),
         16,
         scratch=[
             pltpu.VMEM(objective.shape, jnp.float32),

time: 211 us -> 211 us (level)
  no operation moved by 1% of the time
where the time goes in v3:
time: 211 us; the launch traced here: 210 us
  blocking collectives  189 us (90%)
  Pallas kernels  17.2 us (8%)
  local copies, waits for them, and re-layouts  2.67 us (1%)
    all_to_all x8, blocking collectives, exchange(): return lax.all_to_all(block, 'tm', split_axis=0, concat_axis=0, tiled=True)  189 us
    pallas_call x9, Pallas kernels, call(): pl.pallas_call(kernel, out_shape=out_shape, in_specs=[pl.BlockSpec(memory...  17.2 us

profile of v3, /device:TPU:1, one launch (start us, length us, event | category | flops | bytes accessed | tf_op | source)
XLA Modules:
  0.0 210.2 jit_solution(712768704182924676)
XLA Ops:
  0.6 0.0 copy-start.1
  0.6 1.7 copy-done.1
  2.3 0.9 copy-done.8
  3.3 1.1 shard_map.131
  4.4 27.5 %all_to_all.40.refs_0_ = bf16[32,3,8,768]{3,2,1,0:T(8,128)(2,1)S(1)} all-to-all(bf16[32,3,8,768]{3,2,1,0:T(8,128)(2,1)S(1)} %get-tuple-element.4), channel_id=1, replica_groups=mesh['tm'=32,'obj'=4] {'tm'}, dimensions={0} | all-to-all | bytes 2359296 | tf_op jit(solution)/shard_map/all_to_all | solution.py:222
  31.9 0.8 shard_map.132
  32.7 0.0 slice-start
  32.7 22.7 %all_to_all.41.in_ref = bf16[32,3,8,768]{3,2,1,0:T(8,128)(2,1)S(1)} all-to-all(bf16[32,3,8,768]{3,2,1,0:T(8,128)(2,1)S(1)} %shard_map.132), channel_id=1, replica_groups=mesh['tm'=32,'obj'=4] {'tm'}, dimensions={0} | all-to-all | bytes 2359296 | tf_op jit(solution)/shard_map/all_to_all | solution.py:222
  55.4 0.0 copy-done
  55.4 0.0 copy-done.4
  55.4 0.0 slice-start.1
  55.4 3.2 %shard_map.133 = bf16[32,3,8,768]{3,2,1,0:T(8,128)(2,1)S(1)} custom-call(bf16[32,3,8,768]{3,2,1,0:T(8,128)(2,1)S(1)} %all_to_all.41.in_ref, bf16[256,256]{1,0:T(8,128)(2,1)S(1)} %copy-done.3, bf16[256,256]{1,0:T(8,128)(2,1)S(1)} %copy-done.4, bf16[2,4,768,768]{3,2,1,0:T(8,128)(2,1)S(1)} %copy-done), custom_call_target="tpu_custom_call" | custom-call | flops 2147483648 | bytes 4194304 | tf_op jit(solution)/shard_map/pallas_call | solution.py:210
  58.7 0.0 copy-start.7
  58.7 22.6 %all_to_all.42.refs_0_.before_ref = bf16[32,3,8,768]{3,2,1,0:T(8,128)(2,1)S(1)} all-to-all(bf16[32,3,8,768]{3,2,1,0:T(8,128)(2,1)S(1)} %shard_map.133), channel_id=1, replica_groups=mesh['tm'=32,'obj'=4] {'tm'}, dimensions={0} | all-to-all | bytes 2359296 | tf_op jit(solution)/shard_map/all_to_all | solution.py:222
  81.3 0.0 copy-done.7
  81.3 0.8 shard_map.134.refs_1_
  82.1 0.0 copy-start.2
  82.1 22.6 %all_to_all.43.in_ref = bf16[32,3,8,768]{3,2,1,0:T(8,128)(2,1)S(1)} all-to-all(bf16[32,3,8,768]{3,2,1,0:T(8,128)(2,1)S(1)} %shard_map.134.refs_1_), channel_id=1, replica_groups=mesh['tm'=32,'obj'=4] {'tm'}, dimensions={0} | all-to-all | bytes 2359296 | tf_op jit(solution)/shard_map/all_to_all | solution.py:222
  104.7 0.0 slice-done
  104.7 1.8 shard_map.135
  106.5 0.0 copy-start.6
  106.5 22.6 %all_to_all.44.refs_0_ = bf16[32,3,8,768]{3,2,1,0:T(8,128)(2,1)S(1)} all-to-all(bf16[32,3,8,768]{3,2,1,0:T(8,128)(2,1)S(1)} %shard_map.135), channel_id=1, replica_groups=mesh['tm'=32,'obj'=4] {'tm'}, dimensions={0} | all-to-all | bytes 2359296 | tf_op jit(solution)/shard_map/all_to_all | solution.py:222
  129.1 1.4 shard_map.136
  130.5 22.5 %all_to_all.45.in_ref = bf16[32,3,8,768]{3,2,1,0:T(8,128)(2,1)S(1)} all-to-all(bf16[32,3,8,768]{3,2,1,0:T(8,128)(2,1)S(1)} %shard_map.136), channel_id=1, replica_groups=mesh['tm'=32,'obj'=4] {'tm'}, dimensions={0} | all-to-all | bytes 2359296 | tf_op jit(solution)/shard_map/all_to_all | solution.py:222
  153.0 3.2 %shard_map.137 = bf16[32,3,8,768]{3,2,1,0:T(8,128)(2,1)S(1)} custom-call(bf16[32,3,8,768]{3,2,1,0:T(8,128)(2,1)S(1)} %all_to_all.45.in_ref, bf16[256,256]{1,0:T(8,128)(2,1)S(1)} %copy-done.3, bf16[256,256]{1,0:T(8,128)(2,1)S(1)} %copy-done.4, bf16[2,4,768,768]{3,2,1,0:T(8,128)(2,1)S(1)} %copy-done), custom_call_target="tpu_custom_call" | custom-call | flops 2147483648 | bytes 4194304 | tf_op jit(solution)/shard_map/pallas_call | solution.py:210
  156.2 0.0 copy-start.5
  156.2 0.0 copy-start.9
  156.3 22.6 %all_to_all.46.in_ref = bf16[32,3,8,768]{3,2,1,0:T(8,128)(2,1)S(1)} all-to-all(bf16[32,3,8,768]{3,2,1,0:T(8,128)(2,1)S(1)} %shard_map.137), channel_id=1, replica_groups=mesh['tm'=32,'obj'=4] {'tm'}, dimensions={0} | all-to-all | bytes 2359296 | tf_op jit(solution)/shard_map/all_to_all | solution.py:222
  178.9 0.0 copy-done.9
  178.9 2.3 %shard_map.138 = bf16[32,4,8,768]{3,2,1,0:T(8,128)(2,1)S(1)} custom-call(bf16[32,3,8,768]{3,2,1,0:T(8,128)(2,1)S(1)} %all_to_all.42.refs_0_.before_ref, bf16[32,3,8,768]{3,2,1,0:T(8,128)(2,1)S(1)} %all_to_all.46.in_ref, bf16[256,1024]{1,0:T(8,128)(2,1)S(1)} %copy-done.5, bf16[64,1024]{1,0:T(8,128)(2,1)S(1)} %copy-done.9, bf16[256,256]{1,0:T(8,128)(2,1)S(1)} %copy-done.4), custom_call_target="tpu_custom_call" | custom-call | flops 268435456 | bytes 4194304 | tf_op jit(solution)/shard_map/pallas_call | solution.py:210
  181.2 26.3 %all_to_all.47.in_ref = bf16[32,4,8,768]{3,2,1,0:T(8,128)(2,1)S(1)} all-to-all(bf16[32,4,8,768]{3,2,1,0:T(8,128)(2,1)S(1)} %shard_map.138), channel_id=1, replica_groups=mesh['tm'=32,'obj'=4] {'tm'}, dimensions={0} | all-to-all | bytes 3145728 | tf_op jit(solution)/shard_map/all_to_all | solution.py:222
  207.5 2.6 %shard_map.139 = (f32[4,192,768]{2,1,0:T(8,128)}, f32[4,192,768]{2,1,0:T(8,128)}) custom-call(bf16[32,4,8,768]{3,2,1,0:T(8,128)(2,1)S(1)} %all_to_all.47.in_ref, f32[4,192,768]{2,1,0:T(8,128)S(1)} %copy-done.2, bf16[4,768,768]{2,1,0:T(8,128)(2,1)S(1)} %bitcast.1, bf16[256,256]{1,0:T(8,128)(2,1)S(1)} %copy-done.3, bf16[256,256]{1,0:T(8,128)(2,1)S(1)} %copy-done.3), custom_call_target="tpu_custom_call" | custom-call | flops 1073741824 | bytes 4194304 | tf_op jit(solution)/shard_map/pallas_call | solution.py:210
  (10 shorter events, 0.0 us)
Async XLA Ops:
  0.6 1.7 copy-start.1
  2.3 0.9 copy-start.8
  3.2 52.2 %copy-start = (bf16[2,4,768,768]{3,2,1,0:T(8,128)(2,1)S(1)}, bf16[2,4,768,768]{3,2,1,0:T(8,128)(2,1)}, u32[]{:S(2)}) copy-start(bf16[2,4,768,768]{3,2,1,0:T(8,128)(2,1)} %blocks_ref.3) | copy-start | bytes 28311556
  31.9 23.6 %copy-start.3 = (bf16[256,256]{1,0:T(8,128)(2,1)S(1)}, bf16[256,256]{1,0:T(8,128)(2,1)}, u32[]{:S(2)}) copy-start(bf16[256,256]{1,0:T(8,128)(2,1)} %constant.20.clone.sort_ref.unpack_ref) | copy-start | bytes 393220
  31.9 23.6 %copy-start.4 = (bf16[256,256]{1,0:T(8,128)(2,1)S(1)}, bf16[256,256]{1,0:T(8,128)(2,1)}, u32[]{:S(2)}) copy-start(bf16[256,256]{1,0:T(8,128)(2,1)} %constant.19.clone.unsort_ref.pack_ref.spread_ref) | copy-start | bytes 393220
  32.7 72.0 %slice-start = ((s8[4718592]{0:T(1024)(128)(4,1)}), s8[4194304]{0:T(1024)(128)(4,1)S(1)}, s32[]{:S(2)}) async-start(s8[4718592]{0:T(1024)(128)(4,1)} %bitcast), calls=%async_computation.8 | async-start | bytes 8388608
  55.4 49.3 %slice-start.1 = ((s8[4718592]{0:T(1024)(128)(4,1)}), s8[524288]{0:T(1024)(128)(4,1)S(1)}, s32[]{:S(2)}) async-start(s8[4718592]{0:T(1024)(128)(4,1)} %bitcast), calls=%async_computation.9 | async-start | bytes 1048576
  58.7 22.6 %copy-start.7 = (bf16[256,512]{1,0:T(8,128)(2,1)S(1)}, bf16[256,512]{1,0:T(8,128)(2,1)}, u32[]{:S(2)}) copy-start(bf16[256,512]{1,0:T(8,128)(2,1)} %constant.17.clone.refs_1_) | copy-start | bytes 786436
  82.1 22.6 %copy-start.2 = (f32[4,192,768]{2,1,0:T(8,128)S(1)}, f32[4,192,768]{2,1,0:T(8,128)}, u32[]{:S(2)}) copy-start(f32[4,192,768]{2,1,0:T(8,128)} %objective_ref.3) | copy-start | bytes 7077892
  106.5 22.6 %copy-start.6 = (bf16[256,1024]{1,0:T(8,128)(2,1)S(1)}, bf16[256,1024]{1,0:T(8,128)(2,1)}, u32[]{:S(2)}) copy-start(bf16[256,1024]{1,0:T(8,128)(2,1)} %constant.15.clone.refs_2_) | copy-start | bytes 1572868
  156.2 22.6 %copy-start.5 = (bf16[256,1024]{1,0:T(8,128)(2,1)S(1)}, bf16[256,1024]{1,0:T(8,128)(2,1)}, u32[]{:S(2)}) copy-start(bf16[256,1024]{1,0:T(8,128)(2,1)} %constant.16.clone.table_ref) | copy-start | bytes 1572868
  156.2 22.6 %copy-start.9 = (bf16[64,1024]{1,0:T(8,128)(2,1)S(1)}, bf16[64,1024]{1,0:T(8,128)(2,1)}, u32[]{:S(2)}) copy-start(bf16[64,1024]{1,0:T(8,128)(2,1)} %constant.18.clone.beyond_ref) | copy-start | bytes 393220

commit v4 on v3

--- a/solution.py
+++ b/solution.py
@@ -75,8 +75,7 @@
 
 def rows_of(ref, third):
     groups, _, eight, states = ref.shape
-    wide = ref[:, third].astype(jnp.float32)
-    return wide.reshape(groups * eight, states).astype(jnp.bfloat16)
+    return ref[:, third].reshape(groups * eight, states)
 
 
 def put_rows(ref, third, rows):
@@ -84,29 +83,18 @@
     ref[:, third] = rows.reshape(groups, eight, states).astype(ref.dtype)
 
 
-def pack_kernel(objective_hbm, table_hbm, send_ref, table_ref, rows_ref, sem):
+def pack_kernel(objective_ref, send_ref):
     groups, thirds, eight, states = send_ref.shape
-    steps, columns, _ = rows_ref.shape
+    steps, columns, _ = objective_ref.shape
     width = columns // thirds
-    copies = []
-    for third in range(thirds):
-        part = pl.ds(third * width, width)
-        copies.append(
-            pltpu.make_async_copy(objective_hbm.at[:, part], rows_ref.at[:, part], sem.at[third])
-        )
-        copies[-1].start()
-    table_copy = pltpu.make_async_copy(table_hbm, table_ref, sem.at[thirds])
-    table_copy.start()
     shape = (eight * groups, eight * groups)
     row = lax.broadcasted_iota(jnp.int32, shape, 0)
     source = (row % steps) * width + (row // steps % 2) * groups + row // eight
     pack = (source == lax.broadcasted_iota(jnp.int32, shape, 1)).astype(jnp.float32)
     pack = pack.astype(jnp.bfloat16)
     for third in range(thirds):
-        copies[third].wait()
-        rows = rows_ref[:, third * width : (third + 1) * width].astype(jnp.bfloat16)
+        rows = objective_ref[:, third * width : (third + 1) * width].astype(jnp.bfloat16)
         put_rows(send_ref, third, mul(pack, rows.reshape(steps * width, states)))
-    table_copy.wait()
 
 
 def transform_kernel(*refs):
@@ -118,14 +106,15 @@
         put_rows(out_ref, third, mul(table_ref[...], jnp.concatenate(rows, axis=0)))
 
 
-def last_transform_kernel(before_ref, in_ref, table_ref, beyond_ref, spread_ref, out_ref):
-    groups, thirds = in_ref.shape[:2]
+def last_transform_kernel(before_ref, in_ref, table_ref, spread_ref, out_ref):
+    groups, thirds, eight, _ = in_ref.shape
     extra = []
     for third in range(thirds):
         before, rows = rows_of(before_ref, third), rows_of(in_ref, third)
         rows = jnp.concatenate([before, before, rows, rows], axis=0)
-        extra.append(mul(beyond_ref[...], rows).astype(jnp.bfloat16))
-        put_rows(out_ref, third, mul(table_ref[...], rows))
+        rows = mul(table_ref[...], rows)
+        extra.append(rows[eight * groups :].astype(jnp.bfloat16))
+        put_rows(out_ref, third, rows[: eight * groups])
     extra.append(jnp.zeros_like(extra[0]))
     put_rows(out_ref, thirds, mul(spread_ref[...], jnp.concatenate(extra, axis=0)))
 
@@ -205,12 +194,11 @@
         copy.wait()
 
 
-def call(kernel, out_shape, args, limit, scratch=(), in_space=pltpu.VMEM,
-         out_space=pltpu.VMEM, flops=1 << 28):
+def call(kernel, out_shape, args, limit, scratch=(), out_space=pltpu.VMEM, flops=1 << 28):
     return pl.pallas_call(
         kernel,
         out_shape=out_shape,
-        in_specs=[pl.BlockSpec(memory_space=in_space)] * len(args),
+        in_specs=[pl.BlockSpec(memory_space=pltpu.VMEM)] * len(args),
         out_specs=jax.tree.map(lambda _: pl.BlockSpec(memory_space=out_space), out_shape),
         scratch_shapes=list(scratch),
         compiler_params=pltpu.CompilerParams(vmem_limit_bytes=limit * MIB),
@@ -232,13 +220,13 @@
         split_table(t) for t in (forward, backward, -forward_next, backward_next, beyond)
     )
     second = np.concatenate([forward, subtract_next], axis=1)
-    both = np.concatenate([backward, backward], axis=1)
-    beyond = np.concatenate([beyond, beyond], axis=1)
+    both = np.concatenate([backward, beyond], axis=0)
+    both = np.concatenate([both, both], axis=1)
     pack, sort = shuffles(groups)
     unpack, unsort = pack.T.copy(), sort.T.copy()
-    forward, second, both, backward_next, beyond, pack, unpack, sort, unsort = (
+    forward, second, both, backward_next, pack, unpack, sort, unsort = (
         jnp.asarray(t)
-        for t in (forward, second, both, backward_next, beyond, pack, unpack, sort, unsort)
+        for t in (forward, second, both, backward_next, pack, unpack, sort, unsort)
     )
     wire = jax.ShapeDtypeStruct((groups, thirds, 8, states), jnp.bfloat16)
     longer = jax.ShapeDtypeStruct((groups, thirds + 1, 8, states), jnp.bfloat16)
@@ -254,18 +242,8 @@
             flops=1 << 31,
         )
 
-    send, table = call(
-        pack_kernel,
-        (wire, jax.ShapeDtypeStruct(forward.shape, forward.dtype)),
-        (objective, forward),
-        16,
-        scratch=[
-            pltpu.VMEM(objective.shape, jnp.float32),
-            pltpu.SemaphoreType.DMA((thirds + 1,)),
-        ],
-        in_space=pltpu.HBM,
-    )
-    rows = call(transform_kernel, wire, (exchange(send), table), 16)
+    send = call(pack_kernel, wire, (objective,), 16)
+    rows = call(transform_kernel, wire, (exchange(send), forward), 16)
     wave = exchange(multiply(exchange(rows)))
     ahead = call(transform_kernel, wire, (wave, backward_next), 16)
     send = call(
@@ -278,7 +256,7 @@
     )
     rows = call(transform_kernel, wire, (exchange(send), ahead, second), 16)
     again = exchange(multiply(exchange(rows)))
-    rows = call(last_transform_kernel, longer, (wave, again, both, beyond, unsort), 16)
+    rows = call(last_transform_kernel, longer, (wave, again, both, unsort), 16)
     return call(
         finish_kernel,
         (field, field),

time: 211 us -> 210 us (level)
  no operation moved by 1% of the time
where the time goes in v4:
time: 210 us; the launch traced here: 209 us
  blocking collectives  189 us (90%)
  Pallas kernels  16.2 us (8%)
  local copies, waits for them, and re-layouts  2.66 us (1%)
    all_to_all x8, blocking collectives, exchange(): return lax.all_to_all(block, 'tm', split_axis=0, concat_axis=0, tiled=True)  189 us
    pallas_call x9, Pallas kernels, call(): pl.pallas_call(kernel, out_shape=out_shape, in_specs=[pl.BlockSpec(memory...  16.2 us

profile of v4, /device:TPU:1, one launch (start us, length us, event | category | flops | bytes accessed | tf_op | source)
XLA Modules:
  0.0 209.2 jit_solution(7464011607166228647)
XLA Ops:
  0.6 0.0 copy-start.1
  0.6 1.7 copy-done.1
  2.3 0.5 shard_map.122
  2.8 27.5 %all_to_all.40.refs_0_ = bf16[32,3,8,768]{3,2,1,0:T(8,128)(2,1)S(1)} all-to-all(bf16[32,3,8,768]{3,2,1,0:T(8,128)(2,1)S(1)} %shard_map.122), channel_id=1, replica_groups=mesh['tm'=32,'obj'=4] {'tm'}, dimensions={0} | all-to-all | bytes 2359296 | tf_op jit(solution)/shard_map/all_to_all | solution.py:210
  30.3 0.9 copy-done.8
  31.2 0.8 shard_map.123
  32.0 0.0 slice-start
  32.0 22.7 %all_to_all.41.in_ref = bf16[32,3,8,768]{3,2,1,0:T(8,128)(2,1)S(1)} all-to-all(bf16[32,3,8,768]{3,2,1,0:T(8,128)(2,1)S(1)} %shard_map.123), channel_id=1, replica_groups=mesh['tm'=32,'obj'=4] {'tm'}, dimensions={0} | all-to-all | bytes 2359296 | tf_op jit(solution)/shard_map/all_to_all | solution.py:210
  54.8 0.0 copy-done
  54.8 0.0 copy-done.3
  54.8 0.0 copy-done.4
  54.8 0.0 slice-start.1
  54.8 3.2 %shard_map.124 = bf16[32,3,8,768]{3,2,1,0:T(8,128)(2,1)S(1)} custom-call(bf16[32,3,8,768]{3,2,1,0:T(8,128)(2,1)S(1)} %all_to_all.41.in_ref, bf16[256,256]{1,0:T(8,128)(2,1)S(1)} %copy-done.3, bf16[256,256]{1,0:T(8,128)(2,1)S(1)} %copy-done.4, bf16[2,4,768,768]{3,2,1,0:T(8,128)(2,1)S(1)} %copy-done), custom_call_target="tpu_custom_call" | custom-call | flops 2147483648 | bytes 4194304 | tf_op jit(solution)/shard_map/pallas_call | solution.py:198
  58.0 0.0 copy-start.7
  58.0 22.6 %all_to_all.42.refs_0_.before_ref = bf16[32,3,8,768]{3,2,1,0:T(8,128)(2,1)S(1)} all-to-all(bf16[32,3,8,768]{3,2,1,0:T(8,128)(2,1)S(1)} %shard_map.124), channel_id=1, replica_groups=mesh['tm'=32,'obj'=4] {'tm'}, dimensions={0} | all-to-all | bytes 2359296 | tf_op jit(solution)/shard_map/all_to_all | solution.py:210
  80.6 0.0 copy-done.7
  80.6 0.8 shard_map.125.refs_1_
  81.4 0.0 copy-start.2
  81.4 22.6 %all_to_all.43.in_ref = bf16[32,3,8,768]{3,2,1,0:T(8,128)(2,1)S(1)} all-to-all(bf16[32,3,8,768]{3,2,1,0:T(8,128)(2,1)S(1)} %shard_map.125.refs_1_), channel_id=1, replica_groups=mesh['tm'=32,'obj'=4] {'tm'}, dimensions={0} | all-to-all | bytes 2359296 | tf_op jit(solution)/shard_map/all_to_all | solution.py:210
  104.1 0.0 slice-done.1
  104.1 1.8 shard_map.126
  105.9 0.0 copy-start.6
  105.9 22.6 %all_to_all.44.refs_0_ = bf16[32,3,8,768]{3,2,1,0:T(8,128)(2,1)S(1)} all-to-all(bf16[32,3,8,768]{3,2,1,0:T(8,128)(2,1)S(1)} %shard_map.126), channel_id=1, replica_groups=mesh['tm'=32,'obj'=4] {'tm'}, dimensions={0} | all-to-all | bytes 2359296 | tf_op jit(solution)/shard_map/all_to_all | solution.py:210
  128.5 0.0 copy-done.6
  128.5 1.4 shard_map.127
  129.9 22.5 %all_to_all.45.in_ref = bf16[32,3,8,768]{3,2,1,0:T(8,128)(2,1)S(1)} all-to-all(bf16[32,3,8,768]{3,2,1,0:T(8,128)(2,1)S(1)} %shard_map.127), channel_id=1, replica_groups=mesh['tm'=32,'obj'=4] {'tm'}, dimensions={0} | all-to-all | bytes 2359296 | tf_op jit(solution)/shard_map/all_to_all | solution.py:210
  152.4 3.2 %shard_map.128 = bf16[32,3,8,768]{3,2,1,0:T(8,128)(2,1)S(1)} custom-call(bf16[32,3,8,768]{3,2,1,0:T(8,128)(2,1)S(1)} %all_to_all.45.in_ref, bf16[256,256]{1,0:T(8,128)(2,1)S(1)} %copy-done.3, bf16[256,256]{1,0:T(8,128)(2,1)S(1)} %copy-done.4, bf16[2,4,768,768]{3,2,1,0:T(8,128)(2,1)S(1)} %copy-done), custom_call_target="tpu_custom_call" | custom-call | flops 2147483648 | bytes 4194304 | tf_op jit(solution)/shard_map/pallas_call | solution.py:198
  155.6 0.0 copy-start.5
  155.6 22.6 %all_to_all.46.in_ref = bf16[32,3,8,768]{3,2,1,0:T(8,128)(2,1)S(1)} all-to-all(bf16[32,3,8,768]{3,2,1,0:T(8,128)(2,1)S(1)} %shard_map.128), channel_id=1, replica_groups=mesh['tm'=32,'obj'=4] {'tm'}, dimensions={0} | all-to-all | bytes 2359296 | tf_op jit(solution)/shard_map/all_to_all | solution.py:210
  178.2 2.0 shard_map.129
  180.2 26.3 %all_to_all.47.in_ref = bf16[32,4,8,768]{3,2,1,0:T(8,128)(2,1)S(1)} all-to-all(bf16[32,4,8,768]{3,2,1,0:T(8,128)(2,1)S(1)} %shard_map.129), channel_id=1, replica_groups=mesh['tm'=32,'obj'=4] {'tm'}, dimensions={0} | all-to-all | bytes 3145728 | tf_op jit(solution)/shard_map/all_to_all | solution.py:210
  206.5 2.6 %shard_map.130 = (f32[4,192,768]{2,1,0:T(8,128)}, f32[4,192,768]{2,1,0:T(8,128)}) custom-call(bf16[32,4,8,768]{3,2,1,0:T(8,128)(2,1)S(1)} %all_to_all.47.in_ref, f32[4,192,768]{2,1,0:T(8,128)S(1)} %copy-done.2, bf16[4,768,768]{2,1,0:T(8,128)(2,1)S(1)} %bitcast.1, bf16[256,256]{1,0:T(8,128)(2,1)S(1)} %copy-done.3, bf16[256,256]{1,0:T(8,128)(2,1)S(1)} %copy-done.3), custom_call_target="tpu_custom_call" | custom-call | flops 1073741824 | bytes 4194304 | tf_op jit(solution)/shard_map/pallas_call | solution.py:198
  (8 shorter events, 0.0 us)
Async XLA Ops:
  0.6 1.7 copy-start.1
  2.3 52.5 %copy-start = (bf16[2,4,768,768]{3,2,1,0:T(8,128)(2,1)S(1)}, bf16[2,4,768,768]{3,2,1,0:T(8,128)(2,1)}, u32[]{:S(2)}) copy-start(bf16[2,4,768,768]{3,2,1,0:T(8,128)(2,1)} %blocks_ref.3) | copy-start | bytes 28311556
  30.3 1.0 copy-start.8
  31.2 23.6 %copy-start.3 = (bf16[256,256]{1,0:T(8,128)(2,1)S(1)}, bf16[256,256]{1,0:T(8,128)(2,1)}, u32[]{:S(2)}) copy-start(bf16[256,256]{1,0:T(8,128)(2,1)} %constant.17.clone.sort_ref.unpack_ref) | copy-start | bytes 393220
  31.2 23.6 %copy-start.4 = (bf16[256,256]{1,0:T(8,128)(2,1)S(1)}, bf16[256,256]{1,0:T(8,128)(2,1)}, u32[]{:S(2)}) copy-start(bf16[256,256]{1,0:T(8,128)(2,1)} %constant.16.clone.unsort_ref.pack_ref.spread_ref) | copy-start | bytes 393220
  32.0 72.0 %slice-start = ((s8[4718592]{0:T(1024)(128)(4,1)}), s8[4194304]{0:T(1024)(128)(4,1)S(1)}, s32[]{:S(2)}) async-start(s8[4718592]{0:T(1024)(128)(4,1)} %bitcast), calls=%async_computation.8 | async-start | bytes 8388608
  54.8 49.3 %slice-start.1 = ((s8[4718592]{0:T(1024)(128)(4,1)}), s8[524288]{0:T(1024)(128)(4,1)S(1)}, s32[]{:S(2)}) async-start(s8[4718592]{0:T(1024)(128)(4,1)} %bitcast), calls=%async_computation.9 | async-start | bytes 1048576
  58.0 22.6 %copy-start.7 = (bf16[256,512]{1,0:T(8,128)(2,1)S(1)}, bf16[256,512]{1,0:T(8,128)(2,1)}, u32[]{:S(2)}) copy-start(bf16[256,512]{1,0:T(8,128)(2,1)} %constant.15.clone.refs_1_) | copy-start | bytes 786436
  81.4 22.6 %copy-start.2 = (f32[4,192,768]{2,1,0:T(8,128)S(1)}, f32[4,192,768]{2,1,0:T(8,128)}, u32[]{:S(2)}) copy-start(f32[4,192,768]{2,1,0:T(8,128)} %objective_ref.5) | copy-start | bytes 7077892
  105.9 22.6 %copy-start.6 = (bf16[256,1024]{1,0:T(8,128)(2,1)S(1)}, bf16[256,1024]{1,0:T(8,128)(2,1)}, u32[]{:S(2)}) copy-start(bf16[256,1024]{1,0:T(8,128)(2,1)} %constant.13.clone.refs_2_) | copy-start | bytes 1572868
  155.6 22.6 %copy-start.5 = (bf16[320,1024]{1,0:T(8,128)(2,1)S(1)}, bf16[320,1024]{1,0:T(8,128)(2,1)}, u32[]{:S(2)}) copy-start(bf16[320,1024]{1,0:T(8,128)(2,1)} %constant.14.clone.table_ref) | copy-start | bytes 1966084

commit v5 on v4

--- a/solution.py
+++ b/solution.py
@@ -129,13 +129,15 @@
             sorted_ref[at : at + groups] = rows[block * groups : (block + 1) * groups]
 
     def product(frequency, re_at, im_at, count):
+        re = sorted_ref[re_at : re_at + count]
+        im = sorted_ref[im_at : im_at + count]
         left = jnp.concatenate(
-            [sorted_ref[re_at : re_at + count], sorted_ref[im_at : im_at + count]], axis=0
+            [jnp.concatenate([re, -im], axis=1), jnp.concatenate([im, re], axis=1)], axis=0
         )
-        y = mul(left, blocks_ref[0, frequency])
-        z = mul(left, blocks_ref[1, frequency])
-        sorted_ref[re_at : re_at + count] = (y[:count] - z[count:]).astype(jnp.bfloat16)
-        sorted_ref[im_at : im_at + count] = (z[:count] + y[count:]).astype(jnp.bfloat16)
+        right = jnp.concatenate([blocks_ref[0, frequency], blocks_ref[1, frequency]], axis=0)
+        rows = mul(left, right).astype(jnp.bfloat16)
+        sorted_ref[re_at : re_at + count] = rows[:count]
+        sorted_ref[im_at : im_at + count] = rows[count:]
 
     product(1, 0, 2 * half, 2 * half)
     product(0, 4 * half, 6 * half, half)

time: 210 us -> 209 us (level)
  no operation moved by 1% of the time
where the time goes in v5:
time: 209 us; the launch traced here: 208 us
  blocking collectives  189 us (90%)
  Pallas kernels  15.2 us (7%)
  local copies, waits for them, and re-layouts  2.66 us (1%)
    all_to_all x8, blocking collectives, exchange(): return lax.all_to_all(block, 'tm', split_axis=0, concat_axis=0, tiled=True)  189 us
    pallas_call x9, Pallas kernels, call(): pl.pallas_call(kernel, out_shape=out_shape, in_specs=[pl.BlockSpec(memory...  15.2 us

profile of v5, /device:TPU:1, one launch (start us, length us, event | category | flops | bytes accessed | tf_op | source)
XLA Modules:
  0.0 208.3 jit_solution(4067737325430396101)
XLA Ops:
  0.6 0.0 copy-start.1
  0.6 1.7 copy-done.1
  2.3 0.5 shard_map.122
  2.8 27.5 %all_to_all.40.refs_0_ = bf16[32,3,8,768]{3,2,1,0:T(8,128)(2,1)S(1)} all-to-all(bf16[32,3,8,768]{3,2,1,0:T(8,128)(2,1)S(1)} %shard_map.122), channel_id=1, replica_groups=mesh['tm'=32,'obj'=4] {'tm'}, dimensions={0} | all-to-all | bytes 2359296 | tf_op jit(solution)/shard_map/all_to_all | solution.py:212
  30.3 0.9 copy-done.8
  31.2 0.8 shard_map.123
  32.0 0.0 slice-start
  32.0 22.7 %all_to_all.41.in_ref = bf16[32,3,8,768]{3,2,1,0:T(8,128)(2,1)S(1)} all-to-all(bf16[32,3,8,768]{3,2,1,0:T(8,128)(2,1)S(1)} %shard_map.123), channel_id=1, replica_groups=mesh['tm'=32,'obj'=4] {'tm'}, dimensions={0} | all-to-all | bytes 2359296 | tf_op jit(solution)/shard_map/all_to_all | solution.py:212
  54.8 0.0 copy-done
  54.8 0.0 copy-done.3
  54.8 0.0 copy-done.4
  54.8 0.0 slice-start.1
  54.8 2.7 %shard_map.124 = bf16[32,3,8,768]{3,2,1,0:T(8,128)(2,1)S(1)} custom-call(bf16[32,3,8,768]{3,2,1,0:T(8,128)(2,1)S(1)} %all_to_all.41.in_ref, bf16[256,256]{1,0:T(8,128)(2,1)S(1)} %copy-done.3, bf16[256,256]{1,0:T(8,128)(2,1)S(1)} %copy-done.4, bf16[2,4,768,768]{3,2,1,0:T(8,128)(2,1)S(1)} %copy-done), custom_call_target="tpu_custom_call" | custom-call | flops 2147483648 | bytes 4194304 | tf_op jit(solution)/shard_map/pallas_call | solution.py:200
  57.5 0.0 copy-start.7
  57.5 22.6 %all_to_all.42.refs_0_.before_ref = bf16[32,3,8,768]{3,2,1,0:T(8,128)(2,1)S(1)} all-to-all(bf16[32,3,8,768]{3,2,1,0:T(8,128)(2,1)S(1)} %shard_map.124), channel_id=1, replica_groups=mesh['tm'=32,'obj'=4] {'tm'}, dimensions={0} | all-to-all | bytes 2359296 | tf_op jit(solution)/shard_map/all_to_all | solution.py:212
  80.2 0.0 copy-done.7
  80.2 0.8 shard_map.125.refs_1_
  80.9 0.0 copy-start.2
  81.0 22.6 %all_to_all.43.in_ref = bf16[32,3,8,768]{3,2,1,0:T(8,128)(2,1)S(1)} all-to-all(bf16[32,3,8,768]{3,2,1,0:T(8,128)(2,1)S(1)} %shard_map.125.refs_1_), channel_id=1, replica_groups=mesh['tm'=32,'obj'=4] {'tm'}, dimensions={0} | all-to-all | bytes 2359296 | tf_op jit(solution)/shard_map/all_to_all | solution.py:212
  103.6 0.0 slice-done
  103.6 0.0 slice-done.1
  103.6 1.8 shard_map.126
  105.4 0.0 copy-start.6
  105.4 22.6 %all_to_all.44.refs_0_ = bf16[32,3,8,768]{3,2,1,0:T(8,128)(2,1)S(1)} all-to-all(bf16[32,3,8,768]{3,2,1,0:T(8,128)(2,1)S(1)} %shard_map.126), channel_id=1, replica_groups=mesh['tm'=32,'obj'=4] {'tm'}, dimensions={0} | all-to-all | bytes 2359296 | tf_op jit(solution)/shard_map/all_to_all | solution.py:212
  128.0 1.4 shard_map.127
  129.4 22.5 %all_to_all.45.in_ref = bf16[32,3,8,768]{3,2,1,0:T(8,128)(2,1)S(1)} all-to-all(bf16[32,3,8,768]{3,2,1,0:T(8,128)(2,1)S(1)} %shard_map.127), channel_id=1, replica_groups=mesh['tm'=32,'obj'=4] {'tm'}, dimensions={0} | all-to-all | bytes 2359296 | tf_op jit(solution)/shard_map/all_to_all | solution.py:212
  151.9 2.7 %shard_map.128 = bf16[32,3,8,768]{3,2,1,0:T(8,128)(2,1)S(1)} custom-call(bf16[32,3,8,768]{3,2,1,0:T(8,128)(2,1)S(1)} %all_to_all.45.in_ref, bf16[256,256]{1,0:T(8,128)(2,1)S(1)} %copy-done.3, bf16[256,256]{1,0:T(8,128)(2,1)S(1)} %copy-done.4, bf16[2,4,768,768]{3,2,1,0:T(8,128)(2,1)S(1)} %copy-done), custom_call_target="tpu_custom_call" | custom-call | flops 2147483648 | bytes 4194304 | tf_op jit(solution)/shard_map/pallas_call | solution.py:200
  154.6 0.0 copy-start.5
  154.6 22.6 %all_to_all.46.in_ref = bf16[32,3,8,768]{3,2,1,0:T(8,128)(2,1)S(1)} all-to-all(bf16[32,3,8,768]{3,2,1,0:T(8,128)(2,1)S(1)} %shard_map.128), channel_id=1, replica_groups=mesh['tm'=32,'obj'=4] {'tm'}, dimensions={0} | all-to-all | bytes 2359296 | tf_op jit(solution)/shard_map/all_to_all | solution.py:212
  177.2 2.0 shard_map.129
  179.2 26.3 %all_to_all.47.in_ref = bf16[32,4,8,768]{3,2,1,0:T(8,128)(2,1)S(1)} all-to-all(bf16[32,4,8,768]{3,2,1,0:T(8,128)(2,1)S(1)} %shard_map.129), channel_id=1, replica_groups=mesh['tm'=32,'obj'=4] {'tm'}, dimensions={0} | all-to-all | bytes 3145728 | tf_op jit(solution)/shard_map/all_to_all | solution.py:212
  205.5 2.6 %shard_map.130 = (f32[4,192,768]{2,1,0:T(8,128)}, f32[4,192,768]{2,1,0:T(8,128)}) custom-call(bf16[32,4,8,768]{3,2,1,0:T(8,128)(2,1)S(1)} %all_to_all.47.in_ref, f32[4,192,768]{2,1,0:T(8,128)S(1)} %copy-done.2, bf16[4,768,768]{2,1,0:T(8,128)(2,1)S(1)} %bitcast.1, bf16[256,256]{1,0:T(8,128)(2,1)S(1)} %copy-done.3, bf16[256,256]{1,0:T(8,128)(2,1)S(1)} %copy-done.3), custom_call_target="tpu_custom_call" | custom-call | flops 1073741824 | bytes 4194304 | tf_op jit(solution)/shard_map/pallas_call | solution.py:200
  (8 shorter events, 0.0 us)
Async XLA Ops:
  0.6 1.7 copy-start.1
  2.3 52.5 %copy-start = (bf16[2,4,768,768]{3,2,1,0:T(8,128)(2,1)S(1)}, bf16[2,4,768,768]{3,2,1,0:T(8,128)(2,1)}, u32[]{:S(2)}) copy-start(bf16[2,4,768,768]{3,2,1,0:T(8,128)(2,1)} %blocks_ref.3) | copy-start | bytes 28311556
  30.3 1.0 copy-start.8
  31.2 23.6 %copy-start.3 = (bf16[256,256]{1,0:T(8,128)(2,1)S(1)}, bf16[256,256]{1,0:T(8,128)(2,1)}, u32[]{:S(2)}) copy-start(bf16[256,256]{1,0:T(8,128)(2,1)} %constant.17.clone.sort_ref.unpack_ref) | copy-start | bytes 393220
  31.2 23.6 %copy-start.4 = (bf16[256,256]{1,0:T(8,128)(2,1)S(1)}, bf16[256,256]{1,0:T(8,128)(2,1)}, u32[]{:S(2)}) copy-start(bf16[256,256]{1,0:T(8,128)(2,1)} %constant.16.clone.unsort_ref.pack_ref.spread_ref) | copy-start | bytes 393220
  32.0 71.6 %slice-start = ((s8[4718592]{0:T(1024)(128)(4,1)}), s8[4194304]{0:T(1024)(128)(4,1)S(1)}, s32[]{:S(2)}) async-start(s8[4718592]{0:T(1024)(128)(4,1)} %bitcast), calls=%async_computation.8 | async-start | bytes 8388608
  54.8 48.8 %slice-start.1 = ((s8[4718592]{0:T(1024)(128)(4,1)}), s8[524288]{0:T(1024)(128)(4,1)S(1)}, s32[]{:S(2)}) async-start(s8[4718592]{0:T(1024)(128)(4,1)} %bitcast), calls=%async_computation.9 | async-start | bytes 1048576
  57.5 22.6 %copy-start.7 = (bf16[256,512]{1,0:T(8,128)(2,1)S(1)}, bf16[256,512]{1,0:T(8,128)(2,1)}, u32[]{:S(2)}) copy-start(bf16[256,512]{1,0:T(8,128)(2,1)} %constant.15.clone.refs_1_) | copy-start | bytes 786436
  80.9 22.6 %copy-start.2 = (f32[4,192,768]{2,1,0:T(8,128)S(1)}, f32[4,192,768]{2,1,0:T(8,128)}, u32[]{:S(2)}) copy-start(f32[4,192,768]{2,1,0:T(8,128)} %objective_ref.5) | copy-start | bytes 7077892
  105.4 22.6 %copy-start.6 = (bf16[256,1024]{1,0:T(8,128)(2,1)S(1)}, bf16[256,1024]{1,0:T(8,128)(2,1)}, u32[]{:S(2)}) copy-start(bf16[256,1024]{1,0:T(8,128)(2,1)} %constant.13.clone.refs_2_) | copy-start | bytes 1572868
  154.6 22.6 %copy-start.5 = (bf16[320,1024]{1,0:T(8,128)(2,1)S(1)}, bf16[320,1024]{1,0:T(8,128)(2,1)}, u32[]{:S(2)}) copy-start(bf16[320,1024]{1,0:T(8,128)(2,1)} %constant.14.clone.table_ref) | copy-start | bytes 1966084

commit v6 on v5

--- a/solution.py
+++ b/solution.py
@@ -15,7 +15,7 @@
 def split_table(table):
     high = table.astype(jnp.bfloat16)
     low = (table - high.astype(np.float64)).astype(jnp.bfloat16)
-    return np.concatenate([high, low], axis=1)
+    return np.concatenate([high, low], axis=0)
 
 
 def tables(steps, groups):
@@ -97,22 +97,25 @@
         put_rows(send_ref, third, mul(pack, rows.reshape(steps * width, states)))
 
 
+def apply_table(table_ref, rows):
+    both = mul(table_ref[...], rows)
+    count = both.shape[0] // 2
+    return both[:count] + both[count:]
+
+
 def transform_kernel(*refs):
     *in_refs, table_ref, out_ref = refs
     for third in range(out_ref.shape[1]):
-        rows = []
-        for in_ref in in_refs:
-            rows += [rows_of(in_ref, third)] * 2
-        put_rows(out_ref, third, mul(table_ref[...], jnp.concatenate(rows, axis=0)))
+        rows = [rows_of(in_ref, third) for in_ref in in_refs]
+        put_rows(out_ref, third, apply_table(table_ref, jnp.concatenate(rows, axis=0)))
 
 
 def last_transform_kernel(before_ref, in_ref, table_ref, spread_ref, out_ref):
     groups, thirds, eight, _ = in_ref.shape
     extra = []
     for third in range(thirds):
-        before, rows = rows_of(before_ref, third), rows_of(in_ref, third)
-        rows = jnp.concatenate([before, before, rows, rows], axis=0)
-        rows = mul(table_ref[...], rows)
+        rows = [rows_of(before_ref, third), rows_of(in_ref, third)]
+        rows = apply_table(table_ref, jnp.concatenate(rows, axis=0))
         extra.append(rows[eight * groups :].astype(jnp.bfloat16))
         put_rows(out_ref, third, rows[: eight * groups])
     extra.append(jnp.zeros_like(extra[0]))
@@ -218,12 +221,16 @@
     steps = local_steps * groups
     thirds = columns // (2 * groups)
     forward, backward, forward_next, backward_next, beyond = tables(steps, groups)
-    forward, backward, subtract_next, backward_next, beyond = (
-        split_table(t) for t in (forward, backward, -forward_next, backward_next, beyond)
-    )
-    second = np.concatenate([forward, subtract_next], axis=1)
     both = np.concatenate([backward, beyond], axis=0)
-    both = np.concatenate([both, both], axis=1)
+    forward, second, both, backward_next = (
+        split_table(t)
+        for t in (
+            forward,
+            np.concatenate([forward, -forward_next], axis=1),
+            np.concatenate([both, both], axis=1),
+            backward_next,
+        )
+    )
     pack, sort = shuffles(groups)
     unpack, unsort = pack.T.copy(), sort.T.copy()
     forward, second, both, backward_next, pack, unpack, sort, unsort = (

time: 209 us -> 209 us (level)
  no operation moved by 1% of the time
where the time goes in v6:
time: 209 us; the launch traced here: 208 us
  blocking collectives  189 us (90%)
  Pallas kernels  15.2 us (7%)
  local copies, waits for them, and re-layouts  2.66 us (1%)
    all_to_all x8, blocking collectives, exchange(): return lax.all_to_all(block, 'tm', split_axis=0, concat_axis=0, tiled=True)  189 us
    pallas_call x9, Pallas kernels, call(): pl.pallas_call(kernel, out_shape=out_shape, in_specs=[pl.BlockSpec(memory...  15.2 us

profile of v6, /device:TPU:1, one launch (start us, length us, event | category | flops | bytes accessed | tf_op | source)
XLA Modules:
  0.0 208.3 jit_solution(13850446886000960442)
XLA Ops:
  0.6 0.0 copy-start.1
  0.6 1.7 copy-done.1
  2.3 0.5 shard_map.122
  2.8 27.5 %all_to_all.40.refs_0_ = bf16[32,3,8,768]{3,2,1,0:T(8,128)(2,1)S(1)} all-to-all(bf16[32,3,8,768]{3,2,1,0:T(8,128)(2,1)S(1)} %shard_map.122), channel_id=1, replica_groups=mesh['tm'=32,'obj'=4] {'tm'}, dimensions={0} | all-to-all | bytes 2359296 | tf_op jit(solution)/shard_map/all_to_all | solution.py:215
  30.3 0.9 copy-done.8
  31.2 0.8 shard_map.123
  32.0 0.0 slice-start
  32.0 22.7 %all_to_all.41.in_ref = bf16[32,3,8,768]{3,2,1,0:T(8,128)(2,1)S(1)} all-to-all(bf16[32,3,8,768]{3,2,1,0:T(8,128)(2,1)S(1)} %shard_map.123), channel_id=1, replica_groups=mesh['tm'=32,'obj'=4] {'tm'}, dimensions={0} | all-to-all | bytes 2359296 | tf_op jit(solution)/shard_map/all_to_all | solution.py:215
  54.8 0.0 copy-done
  54.8 0.0 copy-done.3
  54.8 0.0 copy-done.4
  54.8 0.0 slice-start.1
  54.8 2.7 %shard_map.124 = bf16[32,3,8,768]{3,2,1,0:T(8,128)(2,1)S(1)} custom-call(bf16[32,3,8,768]{3,2,1,0:T(8,128)(2,1)S(1)} %all_to_all.41.in_ref, bf16[256,256]{1,0:T(8,128)(2,1)S(1)} %copy-done.3, bf16[256,256]{1,0:T(8,128)(2,1)S(1)} %copy-done.4, bf16[2,4,768,768]{3,2,1,0:T(8,128)(2,1)S(1)} %copy-done), custom_call_target="tpu_custom_call" | custom-call | flops 2147483648 | bytes 4194304 | tf_op jit(solution)/shard_map/pallas_call | solution.py:203
  57.5 0.0 copy-start.7
  57.5 22.6 %all_to_all.42.refs_0_.before_ref = bf16[32,3,8,768]{3,2,1,0:T(8,128)(2,1)S(1)} all-to-all(bf16[32,3,8,768]{3,2,1,0:T(8,128)(2,1)S(1)} %shard_map.124), channel_id=1, replica_groups=mesh['tm'=32,'obj'=4] {'tm'}, dimensions={0} | all-to-all | bytes 2359296 | tf_op jit(solution)/shard_map/all_to_all | solution.py:215
  80.1 0.8 shard_map.125.refs_1_
  80.9 0.0 copy-start.2
  80.9 22.6 %all_to_all.43.in_ref = bf16[32,3,8,768]{3,2,1,0:T(8,128)(2,1)S(1)} all-to-all(bf16[32,3,8,768]{3,2,1,0:T(8,128)(2,1)S(1)} %shard_map.125.refs_1_), channel_id=1, replica_groups=mesh['tm'=32,'obj'=4] {'tm'}, dimensions={0} | all-to-all | bytes 2359296 | tf_op jit(solution)/shard_map/all_to_all | solution.py:215
  103.6 0.0 slice-done
  103.6 1.8 shard_map.126
  105.4 0.0 copy-start.6
  105.4 22.6 %all_to_all.44.refs_0_ = bf16[32,3,8,768]{3,2,1,0:T(8,128)(2,1)S(1)} all-to-all(bf16[32,3,8,768]{3,2,1,0:T(8,128)(2,1)S(1)} %shard_map.126), channel_id=1, replica_groups=mesh['tm'=32,'obj'=4] {'tm'}, dimensions={0} | all-to-all | bytes 2359296 | tf_op jit(solution)/shard_map/all_to_all | solution.py:215
  128.0 0.0 copy-done.6
  128.0 1.4 shard_map.127
  129.4 22.5 %all_to_all.45.in_ref = bf16[32,3,8,768]{3,2,1,0:T(8,128)(2,1)S(1)} all-to-all(bf16[32,3,8,768]{3,2,1,0:T(8,128)(2,1)S(1)} %shard_map.127), channel_id=1, replica_groups=mesh['tm'=32,'obj'=4] {'tm'}, dimensions={0} | all-to-all | bytes 2359296 | tf_op jit(solution)/shard_map/all_to_all | solution.py:215
  151.9 2.7 %shard_map.128 = bf16[32,3,8,768]{3,2,1,0:T(8,128)(2,1)S(1)} custom-call(bf16[32,3,8,768]{3,2,1,0:T(8,128)(2,1)S(1)} %all_to_all.45.in_ref, bf16[256,256]{1,0:T(8,128)(2,1)S(1)} %copy-done.3, bf16[256,256]{1,0:T(8,128)(2,1)S(1)} %copy-done.4, bf16[2,4,768,768]{3,2,1,0:T(8,128)(2,1)S(1)} %copy-done), custom_call_target="tpu_custom_call" | custom-call | flops 2147483648 | bytes 4194304 | tf_op jit(solution)/shard_map/pallas_call | solution.py:203
  154.6 0.0 copy-start.5
  154.6 22.6 %all_to_all.46.in_ref = bf16[32,3,8,768]{3,2,1,0:T(8,128)(2,1)S(1)} all-to-all(bf16[32,3,8,768]{3,2,1,0:T(8,128)(2,1)S(1)} %shard_map.128), channel_id=1, replica_groups=mesh['tm'=32,'obj'=4] {'tm'}, dimensions={0} | all-to-all | bytes 2359296 | tf_op jit(solution)/shard_map/all_to_all | solution.py:215
  177.2 0.0 copy-done.5
  177.2 2.0 shard_map.129
  179.2 26.3 %all_to_all.47.in_ref = bf16[32,4,8,768]{3,2,1,0:T(8,128)(2,1)S(1)} all-to-all(bf16[32,4,8,768]{3,2,1,0:T(8,128)(2,1)S(1)} %shard_map.129), channel_id=1, replica_groups=mesh['tm'=32,'obj'=4] {'tm'}, dimensions={0} | all-to-all | bytes 3145728 | tf_op jit(solution)/shard_map/all_to_all | solution.py:215
  205.5 2.6 %shard_map.130 = (f32[4,192,768]{2,1,0:T(8,128)}, f32[4,192,768]{2,1,0:T(8,128)}) custom-call(bf16[32,4,8,768]{3,2,1,0:T(8,128)(2,1)S(1)} %all_to_all.47.in_ref, f32[4,192,768]{2,1,0:T(8,128)S(1)} %copy-done.2, bf16[4,768,768]{2,1,0:T(8,128)(2,1)S(1)} %bitcast.1, bf16[256,256]{1,0:T(8,128)(2,1)S(1)} %copy-done.3, bf16[256,256]{1,0:T(8,128)(2,1)S(1)} %copy-done.3), custom_call_target="tpu_custom_call" | custom-call | flops 1073741824 | bytes 4194304 | tf_op jit(solution)/shard_map/pallas_call | solution.py:203
  (8 shorter events, 0.0 us)
Async XLA Ops:
  0.6 1.7 copy-start.1
  2.3 52.5 %copy-start = (bf16[2,4,768,768]{3,2,1,0:T(8,128)(2,1)S(1)}, bf16[2,4,768,768]{3,2,1,0:T(8,128)(2,1)}, u32[]{:S(2)}) copy-start(bf16[2,4,768,768]{3,2,1,0:T(8,128)(2,1)} %blocks_ref.3) | copy-start | bytes 28311556
  30.3 1.0 copy-start.8
  31.2 23.5 %copy-start.3 = (bf16[256,256]{1,0:T(8,128)(2,1)S(1)}, bf16[256,256]{1,0:T(8,128)(2,1)}, u32[]{:S(2)}) copy-start(bf16[256,256]{1,0:T(8,128)(2,1)} %constant.17.clone.sort_ref.unpack_ref) | copy-start | bytes 393220
  31.2 23.6 %copy-start.4 = (bf16[256,256]{1,0:T(8,128)(2,1)S(1)}, bf16[256,256]{1,0:T(8,128)(2,1)}, u32[]{:S(2)}) copy-start(bf16[256,256]{1,0:T(8,128)(2,1)} %constant.16.clone.unsort_ref.pack_ref.spread_ref) | copy-start | bytes 393220
  32.0 71.6 %slice-start = ((s8[4718592]{0:T(1024)(128)(4,1)}), s8[4194304]{0:T(1024)(128)(4,1)S(1)}, s32[]{:S(2)}) async-start(s8[4718592]{0:T(1024)(128)(4,1)} %bitcast), calls=%async_computation.8 | async-start | bytes 8388608
  54.8 48.8 %slice-start.1 = ((s8[4718592]{0:T(1024)(128)(4,1)}), s8[524288]{0:T(1024)(128)(4,1)S(1)}, s32[]{:S(2)}) async-start(s8[4718592]{0:T(1024)(128)(4,1)} %bitcast), calls=%async_computation.9 | async-start | bytes 1048576
  57.5 22.6 %copy-start.7 = (bf16[512,256]{1,0:T(8,128)(2,1)S(1)}, bf16[512,256]{1,0:T(8,128)(2,1)}, u32[]{:S(2)}) copy-start(bf16[512,256]{1,0:T(8,128)(2,1)} %constant.15.clone.refs_1_) | copy-start | bytes 786436
  80.9 22.6 %copy-start.2 = (f32[4,192,768]{2,1,0:T(8,128)S(1)}, f32[4,192,768]{2,1,0:T(8,128)}, u32[]{:S(2)}) copy-start(f32[4,192,768]{2,1,0:T(8,128)} %objective_ref.5) | copy-start | bytes 7077892
  105.4 22.6 %copy-start.6 = (bf16[512,512]{1,0:T(8,128)(2,1)S(1)}, bf16[512,512]{1,0:T(8,128)(2,1)}, u32[]{:S(2)}) copy-start(bf16[512,512]{1,0:T(8,128)(2,1)} %constant.13.clone.refs_2_) | copy-start | bytes 1572868
  154.6 22.6 %copy-start.5 = (bf16[640,512]{1,0:T(8,128)(2,1)S(1)}, bf16[640,512]{1,0:T(8,128)(2,1)}, u32[]{:S(2)}) copy-start(bf16[640,512]{1,0:T(8,128)(2,1)} %constant.14.clone.table_ref) | copy-start | bytes 1966084
